TPU v7x, 32 devices: a whole 2x2x4 slice. The times are simulated.
32 devices in a mesh: group: 4 (over z), member: 8 (over y, x, core).
Axes of the slice: x: 2, y: 2, z: 4, core: 2. Of those that a mesh axis runs over, the one named last changes fastest.
Arguments:
- hidden: bfloat16 [6144, 2048], P('group'), may hold values from -6 to 6
- token_slab: int32 [6144, 1], P(('group', 'member')), may hold values from 0 to 31; in each aligned block of 192 rows (0 to 191, 192 to 383, ...) at most 12 rows name the same one
- token_row: int32 [6144], P(('group', 'member')), may hold values from 0 to 8191
- slab_owner: int32 [32], replicated, may hold values from 0 to 31, each once
- ple_table: bfloat16 [262144, 256], P(('group', 'member')), may hold values from -0.375 to 0.375
- norm_gains: float32 [1, 3, 2048], replicated, may hold values from 0.1 to 1.9
- w_gate: bfloat16 [1, 2048, 8192], P(None, None, 'member'), may hold values from -0.125 to 0.125
- w_up: bfloat16 [1, 2048, 8192], P(None, None, 'member'), may hold values from -0.125 to 0.125
- w_down: bfloat16 [1, 8192, 2048], P(None, 'member'), may hold values from -0.0625 to 0.0625
- ple_gate: bfloat16 [1, 2048, 256], P(None, None, 'member'), may hold values from -0.125 to 0.125
- ple_proj: bfloat16 [1, 256, 2048], P(None, 'member'), may hold values from -0.375 to 0.375
Outputs:
- hidden_out: bfloat16 [6144, 2048], P('group')
Inputs may be any that keep to these rules, and one draw needn't show every extreme that they name: Within the 192 tokens of one device (aligned blocks of token_slab), no slab is named by more than 12 tokens. Each number appears once: slab s is stored in rows slab_owner[s] * 8192 to slab_owner[s] * 8192 + 8191 of ple_table.
All inputs are finite; a program needn't handle non-finite values.
Results may differ from a plain program's by a relative error of at most 0.0061.
Values may be sent and summed in bfloat16 or wider, within the bound.
No kernel may reach another device: no remote copies, remote signals or barrier semaphores. Data moves between devices by JAX's collectives and lax.ppermute only.
A program may use at most 128 MiB of HBM per device.

v0:
```python
import jax
import jax.numpy as jnp
from jax import lax
from jax.sharding import PartitionSpec as P

PLE = 256


epsilon = 1e-06


def norm_rows(values, scales):
    return values * lax.rsqrt(jnp.mean(values * values, axis=-1, keepdims=True) + epsilon) * scales


def lookup_rows(wanted, ple_table):
    flat_ids = wanted.reshape(-1) - 1
    one_hot = (
        flat_ids[:, None] == jnp.arange(ple_table.shape[0], dtype=jnp.int32)[None, :]
    ).astype(jnp.bfloat16)
    served = jnp.dot(one_hot, ple_table, preferred_element_type=jnp.float32).astype(jnp.bfloat16)
    return served.reshape(wanted.shape + (ple_table.shape[1],))


def request_slots(slab_ids, token_row, slab_owner, devices, slots):
    target = slab_owner[slab_ids]
    order = jnp.arange(token_row.shape[0], dtype=jnp.int32)
    earlier = (target[None, :] == target[:, None]) & (order[None, :] < order[:, None])
    slot_of = jnp.sum(earlier.astype(jnp.int32), axis=1)
    hit_map = (target[:, None, None] == jnp.arange(devices, dtype=jnp.int32)[None, :, None]) & (
        slot_of[:, None, None] == jnp.arange(slots, dtype=jnp.int32)[None, None, :]
    )
    requests = jnp.sum(jnp.where(hit_map, token_row[:, None, None] + 1, 0), axis=0)
    return (hit_map, requests)


def pick_rows(hit_map, returned):
    return jnp.einsum(
        "tdc,dcw->tw", hit_map.astype(jnp.bfloat16), returned, preferred_element_type=jnp.float32
    ).astype(jnp.bfloat16)


def combine_branch(current, partial_value, scales):
    share = lax.psum_scatter(partial_value, "member", scatter_dimension=1, tiled=True)
    share_width = share.shape[1]
    offset = lax.axis_index("member") * share_width
    squares = lax.psum(jnp.sum(share * share, axis=-1, keepdims=True), "member")
    normed = (
        share
        * lax.rsqrt(squares / (share_width * lax.axis_size("member")) + epsilon)
        * lax.dynamic_slice_in_dim(scales, offset, share_width, 0)
    )
    updated = lax.dynamic_slice_in_dim(current, offset, share_width, 1) + normed
    return lax.all_gather(updated, "member", axis=1, tiled=True)


def per_device(
    hidden,
    token_slab,
    token_row,
    slab_owner,
    ple_table,
    norm_gains,
    w_gate,
    w_up,
    w_down,
    ple_gate,
    ple_proj,
):
    members = lax.axis_size("member")
    devices = lax.axis_size("group") * members
    tokens_here = token_row.shape[0]
    slots = max(2, (2 * tokens_here + devices - 1) // devices)
    slab_ids = token_slab[:, 0]
    hit_map, requests = request_slots(slab_ids, token_row, slab_owner, devices, slots)
    grouped = requests.reshape(lax.axis_size("group"), members, slots)
    received = lax.all_to_all(
        lax.all_to_all(grouped, "group", split_axis=0, concat_axis=0, tiled=True),
        "member",
        split_axis=1,
        concat_axis=1,
        tiled=True,
    )
    served = lookup_rows(received, ple_table)
    returned = lax.all_to_all(
        lax.all_to_all(served, "group", split_axis=0, concat_axis=0, tiled=True),
        "member",
        split_axis=1,
        concat_axis=1,
        tiled=True,
    )
    own_rows = pick_rows(hit_map, returned.reshape(devices, slots, ple_table.shape[1]))
    per_member = ple_gate.shape[2]
    layers = w_gate.shape[0]
    pieces = own_rows.reshape(tokens_here, layers, members, per_member)
    columns = lax.all_to_all(pieces, "member", split_axis=2, concat_axis=0, tiled=True)
    ple_part = columns.reshape(-1, layers, per_member).astype(jnp.float32) * PLE**0.5
    current = hidden.astype(jnp.float32)
    normed = norm_rows(current, norm_gains[0, 0]).astype(jnp.bfloat16)
    gate_part = jnp.dot(normed, w_gate[0], preferred_element_type=jnp.float32)
    up_part = jnp.dot(normed, w_up[0], preferred_element_type=jnp.float32)
    activated = (jax.nn.gelu(gate_part, approximate=True) * up_part).astype(jnp.bfloat16)
    mlp_out = jnp.dot(activated, w_down[0], preferred_element_type=jnp.float32)
    current = combine_branch(current, mlp_out, norm_gains[0, 1])
    current_b = current.astype(jnp.bfloat16)
    ple_gate_out = jnp.dot(current_b, ple_gate[0], preferred_element_type=jnp.float32)
    ple_act = (jax.nn.gelu(ple_gate_out, approximate=True) * ple_part[:, 0, :]).astype(jnp.bfloat16)
    ple_out = jnp.dot(ple_act, ple_proj[0], preferred_element_type=jnp.float32)
    current = combine_branch(current, ple_out, norm_gains[0, 2])
    return current.astype(jnp.bfloat16)


def solution(mesh):
    return jax.shard_map(
        per_device,
        mesh=mesh,
        in_specs=(
            P("group", None),
            P(("group", "member"), None),
            P(("group", "member")),
            P(),
            P(("group", "member"), None),
            P(),
            P(None, None, "member"),
            P(None, None, "member"),
            P(None, "member", None),
            P(None, None, "member"),
            P(None, "member", None),
        ),
        out_specs=P("group", None),
        check_vma=False,
    )
```

profile of v0, /device:TPU:0, one launch (start us, length us, event | category | flops | bytes accessed | tf_op | source)
XLA Modules:
  0.0 417.3 jit_solution(211991118664863560)
XLA Ops:
  6.5 4.2 %multiply_reduce_fusion = f32[1536]{0:T(1024)S(1)} fusion(bf16[1536,2048]{1,0:T(8,128)(2,1)} %param.11), kind=kLoop, calls=%fused_computation.2 | loop fusion | flops 9435648 | bytes 6297600 | tf_op jit(solution)/shard_map/reduce_sum | solution.py:13
  11.2 10.4 %fusion.17 = f32[1536,1024]{1,0:T(8,128)} fusion(bf16[1,2048,1024]{2,1,0:T(8,128)(2,1)} %param.17, f32[2048]{0:T(1024)S(1)} %bitcast.75, f32[1536]{0:T(1024)S(1)} %add_rsqrt_fusion, bf16[1536,2048]{1,0:T(8,128)(2,1)S(1)} %copy-done.1), kind=kOutput, calls=%fused_computation.20 | convolution fusion | flops 6455033856 | bytes 16791552 | tf_op jit(solution)/shard_map/dot_general | solution.py:100
  21.6 22.6 %fusion.13 = f32[1536,2048]{1,0:T(8,128)} fusion(bf16[1,1024,2048]{2,1,0:T(8,128)(2,1)} %param.19, f32[1536,1024]{1,0:T(8,128)} %fusion.17, bf16[1,2048,1024]{2,1,0:T(8,128)(2,1)} %param.18, f32[2048]{0:T(1024)S(1)} %bitcast.76, f32[1536]{0:T(1024)S(1)} %add_rsqrt_fusion, bf16[1536,2048]{1,0:T(8,128)(2,1)} %param.11), kind=kOutput, calls=%fused_computation.17 | convolution fusion | flops 12913213440 | bytes 33568768 | tf_op jit(solution)/shard_map/dot_general | solution.py:103
  44.5 9.5 %convert_element_type.38 = f32[1536,2048]{1,0:T(8,128)} convert(bf16[1536,2048]{1,0:T(8,128)(2,1)} %param.11) | non-fusion elementwise | flops 3145728 | bytes 18874368 | tf_op jit(solution)/shard_map/convert_element_type | solution.py:98
  54.0 85.1 %reduce-scatter.3.cloned.1.call-done = f32[1536,256]{1,0:T(8,128)} async-done(((f32[1536,2048]{1,0:T(8,128)}), f32[1536,256]{1,0:T(8,128)}) %reduce-scatter.3.cloned.1.call-update) | async-done | bytes 1572880 | tf_op jit(solution)/shard_map/reduce_scatter | solution.py:44
  139.1 1.7 multiply_reduce_fusion.2
  140.8 12.8 %psum.14 = f32[1536,1]{0,1:T(1,128)S(1)} all-reduce(f32[1536,1]{0,1:T(1,128)S(1)} %broadcast_in_dim.12), channel_id=1, replica_groups=mesh['group'=4,'member'=8] {'member'}, use_global_device_ids=true, to_apply=%region_3.4 | all-reduce | flops 1536 | bytes 12288 | tf_op jit(solution)/shard_map/psum | solution.py:47
  153.6 3.3 multiply_add_fusion.1
  158.4 4.3 %compare_select_fusion.1 = (s32[192,1]{0,1:T(1,128)S(1)}, s32[192,1]{0,1:T(1,128)S(1)}) fusion(s32[]{:T(128)} %bitcast.31, s32[]{:T(128)} %bitcast.32, s32[]{:T(128)} %bitcast.33, s32[]{:T(128)} %bitcast.34, s32[]{:T(128)} %bitcast.35, s32[]{:T(128)} %bitcast.37, s32[]{:T(128)} %bitcast.36, s32[192,1]{0,1:T(1,128)S(1)} %copy-done.6), kind=kLoop, calls=%fused_computation.93 | loop fusion | flops 2880 | bytes 2332 | tf_op jit(solution)/shard_map/gather | solution.py:26
  162.8 15.6 %select_select_fusion = s32[192]{0:T(256)S(1)} fusion(pred[192]{0:T(512)(128)(4,1)S(1)} %get-tuple-element.29, pred[192]{0:T(512)(128)(4,1)S(1)} %get-tuple-element.28, pred[192]{0:T(512)(128)(4,1)S(1)} %get-tuple-element.27, pred[192]{0:T(512)(128)(4,1)S(1)} %get-tuple-element.26, pred[192]{0:T(512)(128)(4,1)S(1)} %get-tuple-element.25, ...), kind=kLoop, calls=%fused_computation.99 | loop fusion | flops 4800 | bytes 6436 | tf_op jit(solution)/shard_map/gather | solution.py:26
  179.1 10.0 %all_to_all.29 = s32[4,8,12]{2,1,0:T(8,128)S(1)} all-to-all(s32[4,8,12]{2,1,0:T(8,128)S(1)} %bitcast.74), channel_id=1, replica_groups=mesh['group'=4,'member'=8] {'group'}, dimensions={0} | all-to-all | bytes 3072 | tf_op jit(solution)/shard_map/all_to_all | solution.py:78
  189.0 7.6 %all_to_all.30 = s32[4,8,12]{2,0,1:T(4,128)S(1)} all-to-all(s32[4,8,12]{2,0,1:T(4,128)S(1)} %copy.43), channel_id=1, replica_groups=mesh['group'=4,'member'=8] {'member'}, dimensions={1} | all-to-all | bytes 3072 | tf_op jit(solution)/shard_map/all_to_all | solution.py:77
  196.8 4.6 %fusion.23 = bf16[384,256]{1,0:T(8,128)(2,1)S(1)} fusion(bf16[8192,256]{1,0:T(8,128)(2,1)} %param.15, s32[384]{0:T(512)S(1)} %sub.7), kind=kOutput, calls=%fused_computation.30 | convolution fusion | flops 1613856768 | bytes 4392448 | tf_op jit(solution)/shard_map/dot_general | solution.py:21
  201.5 10.0 %all_to_all.31 = bf16[4,8,12,256]{3,1,2,0:T(8,128)(2,1)S(1)} all-to-all(bf16[4,8,12,256]{3,1,2,0:T(8,128)(2,1)S(1)} %copy.45), channel_id=1, replica_groups=mesh['group'=4,'member'=8] {'group'}, dimensions={0} | all-to-all | bytes 393216 | tf_op jit(solution)/shard_map/all_to_all | solution.py:86
  211.7 11.1 %all_to_all.32 = bf16[4,8,12,256]{3,0,2,1:T(4,128)(2,1)S(1)} all-to-all(bf16[4,8,12,256]{3,0,2,1:T(4,128)(2,1)S(1)} %copy.46), channel_id=1, replica_groups=mesh['group'=4,'member'=8] {'member'}, dimensions={1} | all-to-all | bytes 393216 | tf_op jit(solution)/shard_map/all_to_all | solution.py:85
  223.2 8.2 %all_to_all.33 = bf16[192,1,8,32]{0,3,1,2:T(8,128)(2,1)S(1)} all-to-all(bf16[192,1,8,32]{0,3,1,2:T(8,128)(2,1)S(1)} %bitcast.73), channel_id=1, replica_groups=mesh['group'=4,'member'=8] {'member'}, dimensions={2} | all-to-all | bytes 196608 | tf_op jit(solution)/shard_map/all_to_all | solution.py:96
  231.7 2.3 all-gather.3.cloned.1.call-done
  234.0 12.7 %fusion.43 = f32[1536,2048]{1,0:T(8,128)} fusion(f32[1536,32]{0,1:T(8,128)S(1)} %mul.170, f32[1536,2048]{1,0:T(8,128)} %all-gather.3.cloned.1.call-done, bf16[1,32,2048]{2,1,0:T(8,128)(2,1)S(1)} %copy-done, bf16[1,2048,32]{1,2,0:T(8,128)(2,1)S(1)} %copy-done.3), kind=kOutput, calls=%fused_computation.47 | convolution fusion | flops 406290432 | bytes 25624576 | tf_op jit(solution)/shard_map/dot_general | solution.py:108
  246.8 93.1 %reduce-scatter.5.cloned.1.call-done = f32[1536,256]{1,0:T(8,128)} async-done(((f32[1536,2048]{1,0:T(8,128)}), f32[1536,256]{1,0:T(8,128)}) %reduce-scatter.5.cloned.1.call-update) | async-done | bytes 1572880 | tf_op jit(solution)/shard_map/reduce_scatter | solution.py:44
  339.8 1.7 multiply_reduce_fusion.1
  341.5 12.8 %psum.15 = f32[1536,1]{0,1:T(1,128)S(1)} all-reduce(f32[1536,1]{0,1:T(1,128)S(1)} %broadcast_in_dim.19), channel_id=1, replica_groups=mesh['group'=4,'member'=8] {'member'}, use_global_device_ids=true, to_apply=%region_8.9 | all-reduce | flops 1536 | bytes 12288 | tf_op jit(solution)/shard_map/psum | solution.py:47
  354.4 3.0 multiply_add_fusion
  357.4 46.7 %all-gather.5.cloned.1.call-done = bf16[1536,2048]{1,0:T(8,128)(2,1)} async-done(((bf16[1536,256]{1,0:T(8,128)(2,1)}), bf16[1536,2048]{1,0:T(8,128)(2,1)}) %all-gather.5.cloned.1.call-update) | async-done | bytes 6291472 | tf_op jit(solution)/shard_map/all_gather | solution.py:54
  404.1 6.6 %copy.57 = bf16[1536,2048]{1,0:T(8,128)(2,1)} copy(bf16[1536,2048]{1,0:T(8,128)(2,1)} %all-gather.5.cloned.1.call-done) | data formatting | bytes 12582912
  (50 shorter events, 4.0 us)
Async XLA Ops:
  6.5 227.5 %copy-start = (bf16[1,32,2048]{2,1,0:T(8,128)(2,1)S(1)}, bf16[1,32,2048]{2,1,0:T(8,128)(2,1)}, u32[]{:S(2)}) copy-start(bf16[1,32,2048]{2,1,0:T(8,128)(2,1)} %param.21) | copy-start | bytes 393220
  6.5 4.3 %copy-start.4 = (f32[1,3,2048]{2,0,1:T(1,128)S(1)}, f32[1,3,2048]{2,0,1:T(1,128)}, u32[]{:S(2)}) copy-start(f32[1,3,2048]{2,0,1:T(1,128)} %param.16) | copy-start | bytes 73732
  6.5 132.5 %reduce-scatter.3.cloned.1.call-start = ((), (), s32[]{:S(2)}) async-start(), calls=%async_computation.7 | async-start | bytes 14155776 | tf_op jit(solution)/shard_map/reduce_scatter | solution.py:44
  6.5 4.6 %copy-start.1 = (bf16[1536,2048]{1,0:T(8,128)(2,1)S(1)}, bf16[1536,2048]{1,0:T(8,128)(2,1)}, u32[]{:S(2)}) copy-start(bf16[1536,2048]{1,0:T(8,128)(2,1)} %param.11) | copy-start | bytes 18874372
  44.2 189.8 %all-gather.3.cloned.1.call-start = ((), (), s32[]{:S(2)}) async-start(), calls=%async_computation.8 | async-start | bytes 14155776 | tf_op jit(solution)/shard_map/all_gather | solution.py:54
  54.0 103.0 %copy-start.2 = (s32[32]{0:T(128)S(1)}, s32[32]{0:T(128)}, u32[]{:S(2)}) copy-start(s32[32]{0:T(128)} %param.14) | copy-start | bytes 388
  54.0 104.4 %copy-start.6 = (s32[192,1]{0,1:T(1,128)S(1)}, s32[192,1]{0,1:T(1,128)}, u32[]{:S(2)}) copy-start(s32[192,1]{0,1:T(1,128)} %param.12) | copy-start | bytes 2308
  54.0 124.6 %copy-start.5 = (s32[192]{0:T(256)S(1)}, s32[192]{0:T(256)}, u32[]{:S(2)}) copy-start(s32[192]{0:T(256)} %param.13) | copy-start | bytes 2308
  156.9 182.9 %reduce-scatter.5.cloned.1.call-start = ((), (), s32[]{:S(2)}) async-start(), calls=%async_computation.9 | async-start | bytes 14155776 | tf_op jit(solution)/shard_map/reduce_scatter | solution.py:44
  196.8 37.2 %copy-start.3 = (bf16[1,2048,32]{1,2,0:T(8,128)(2,1)S(1)}, bf16[1,2048,32]{1,2,0:T(8,128)(2,1)}, u32[]{:S(2)}) copy-start(bf16[1,2048,32]{1,2,0:T(8,128)(2,1)} %param.20) | copy-start | bytes 393220
  246.7 157.4 %all-gather.5.cloned.1.call-start = ((), (), s32[]{:S(2)}) async-start(), calls=%async_computation.10 | async-start | bytes 7077888 | tf_op jit(solution)/shard_map/all_gather | solution.py:54
Sparse Core Ops, SparseCore 0:
  44.4 94.6 reduce-scatter.2
  157.0 76.9 all-gather.2
  246.8 92.9 reduce-scatter.4
  357.5 46.5 all-gather.4
where the time goes:
time: 418 us; the launch traced here: 417 us
  waiting for transfers between devices  227 us (54%)
  blocking collectives  72.4 us (17%)
  matrix products  50.5 us (12%)
  other arithmetic  44 us (11%)
  between operations  13.4 us (3%)
  local copies, waits for them, and re-layouts  9.3 us (2%)
    reduce_scatter x2, waiting for transfers between devices, combine_branch(): lax.psum_scatter(partial_value, 'member', scatter_dimension=1, tiled=True)  178 us
    all_gather x2, waiting for transfers between devices, combine_branch(): return lax.all_gather(updated, 'member', axis=1, tiled=True)  49.1 us
    psum x2, blocking collectives, combine_branch(): squares = lax.psum(jnp.sum(share * share, axis=-1, keepdims=True), 'member')  25.5 us
    dot_general x1, matrix products, per_device(): mlp_out = jnp.dot(activated, w_down[0], preferred_element_type=jnp.float32)  22.6 us
    gather x3, other arithmetic, request_slots(): target = slab_owner[slab_ids]  20 us
    dot_general x1, matrix products, per_device(): ple_out = jnp.dot(ple_act, ple_proj[0], preferred_element_type=jnp.float32)  12.7 us
    all_to_all x1, blocking collectives, per_device(): lax.all_to_all(lax.all_to_all(served, 'group', split_axis=0, concat_axis=...  11.1 us
    dot_general x1, matrix products, per_device(): gate_part = jnp.dot(normed, w_gate[0], preferred_element_type=jnp.float32)  10.4 us
  transfers between devices with their start and end apart: 4, of which 4 were waited for; matrix products, arithmetic and copies ran while one was open for 9% of the time, Pallas kernels for 0%

commit v1 on v0

v1 whole, which is shorter than its diff:
```python
import functools

import jax
import jax.numpy as jnp
from jax import lax
from jax.experimental import pallas as pl
from jax.experimental.pallas import tpu as pltpu
from jax.sharding import PartitionSpec as P


PLE = 256
CHUNKS = 2

epsilon = 1e-06


def gelu(v):
    return 0.5 * v * (1.0 + jnp.tanh(0.7978845608028654 * (v + 0.044715 * (v * v * v))))


def norm_rows(values, scales):
    return values * lax.rsqrt(jnp.mean(values * values, axis=-1, keepdims=True) + epsilon) * scales


def block_order(members):
    near = members.bit_length() - 3
    return sorted(range(members), key=lambda r: ([(r >> b) & 1 for b in range(near)], r))


def mlp_body(
    me, hidden, gains, w_gate, w_up, w_down, keep, send,
    rows, gate_w, up_w, down_w, act, result, in_sems, gate_sems, up_sems, down_sems, out_sems,
    *, order, first, count, parts,
):
    members = len(order)
    half = members // 2
    tiles, _, tile = gate_w.shape
    out_tiles, _, out_tile = down_w.shape

    def fetch(i):
        return pltpu.make_async_copy(
            hidden.at[order[i] ^ me[0], pl.ds(first, count), :], rows.at[i], in_sems.at[i]
        )

    def weights(j):
        return (
            pltpu.make_async_copy(w_gate.at[:, pl.ds(j * tile, tile)], gate_w.at[j], gate_sems.at[j]),
            pltpu.make_async_copy(w_up.at[:, pl.ds(j * tile, tile)], up_w.at[j], up_sems.at[j]),
        )

    def down(j):
        return pltpu.make_async_copy(w_down.at[:, pl.ds(j * out_tile, out_tile)], down_w.at[j], down_sems.at[j])

    def put(j, part):
        return pltpu.make_async_copy(
            result.at[j, pl.ds(part * half, half)],
            (keep, send)[part].at[:, :, pl.ds(j * out_tile, out_tile)],
            out_sems.at[j, part],
        )

    for i in range(members):
        fetch(i).start()
    for j in range(tiles):
        for copy in weights(j):
            copy.start()
    for j in range(out_tiles):
        down(j).start()
    for i in range(members):
        fetch(i).wait()
        rows[i] = norm_rows(rows[i].astype(jnp.float32), gains[...]).astype(jnp.bfloat16)
    per = members // parts
    size = per * count
    for j in range(tiles):
        for copy in weights(j):
            copy.wait()
        for part in range(parts):
            x = rows[part * per : (part + 1) * per].reshape(size, rows.shape[2])
            gate = jnp.dot(x, gate_w[j], preferred_element_type=jnp.float32)
            up = jnp.dot(x, up_w[j], preferred_element_type=jnp.float32)
            act[j, part * size : (part + 1) * size, :] = (gelu(gate) * up).astype(jnp.bfloat16)
    for j in range(out_tiles):
        down(j).wait()
        for part in range(parts):
            total = None
            for k in range(tiles):
                piece = jnp.dot(
                    act[k, part * size : (part + 1) * size, :],
                    down_w[j, k * tile : (k + 1) * tile, :],
                    preferred_element_type=jnp.float32,
                )
                total = piece if total is None else total + piece
            result[j, part * per : (part + 1) * per] = total.reshape(per, count, out_tile).astype(result.dtype)
        put(j, 0).start()
        put(j, 1).start()
    for j in range(out_tiles):
        put(j, 0).wait()
        put(j, 1).wait()


def mlp_chunk(me, hidden, gains, w_gate, w_up, w_down, chunk, count, tile=512, out_tile=512, parts=2):
    members, _, width = hidden.shape
    units = w_gate.shape[1]
    order = block_order(members)
    half = members // 2
    tile = min(tile, units)
    tiles = units // tile
    out_tile = min(out_tile, width)
    out_tiles = width // out_tile
    out = jax.ShapeDtypeStruct((half, count, width), jnp.bfloat16)
    anywhere = pl.BlockSpec(memory_space=pl.ANY)
    return pl.pallas_call(
        functools.partial(mlp_body, order=order, first=chunk * count, count=count, parts=parts),
        out_shape=(out, out),
        in_specs=[pl.BlockSpec(memory_space=pltpu.SMEM), anywhere, pl.BlockSpec(memory_space=pltpu.VMEM)] + [anywhere] * 3,
        out_specs=[anywhere, anywhere],
        scratch_shapes=[
            pltpu.VMEM((members, count, width), jnp.bfloat16),
            pltpu.VMEM((tiles, width, tile), jnp.bfloat16),
            pltpu.VMEM((tiles, width, tile), jnp.bfloat16),
            pltpu.VMEM((out_tiles, units, out_tile), jnp.bfloat16),
            pltpu.VMEM((tiles, members * count, tile), jnp.bfloat16),
            pltpu.VMEM((out_tiles, members, count, out_tile), jnp.bfloat16),
            pltpu.SemaphoreType.DMA((members,)),
            pltpu.SemaphoreType.DMA((tiles,)),
            pltpu.SemaphoreType.DMA((tiles,)),
            pltpu.SemaphoreType.DMA((out_tiles,)),
            pltpu.SemaphoreType.DMA((out_tiles, 2)),
        ],
        compiler_params=pltpu.CompilerParams(vmem_limit_bytes=48 << 20),
        cost_estimate=pl.CostEstimate(
            flops=6 * members * count * width * units,
            bytes_accessed=6 * width * units,
            transcendentals=members * count * units,
        ),
        name="mlp",
    )(me, hidden, gains, w_gate, w_up, w_down)


def ple_body(me, keep, recv, from_x, from_y, hidden, gains, looked, mine, mate, out, weights, sems, *, order):
    half, _, share, _ = mine.shape
    members = 2 * half

    def fetch(j, source):
        relative = j ^ me[0]
        place = sum(((relative >> bit) & 1) << i for i, bit in enumerate(order[:-1]))
        return pltpu.make_async_copy(
            source.at[place], weights.at[:, pl.ds(j * share, share), :], sems.at[j]
        )

    for j in range(members):
        other = ((j ^ me[0]) >> order[-1]) & 1

        @pl.when(other == 0)
        def _():
            fetch(j, mine).start()

        @pl.when(other == 1)
        def _():
            fetch(j, mate).start()

    f32 = jnp.float32
    branch = keep[0].astype(f32) + recv[0].astype(f32) + from_x[...].astype(f32) + from_y[...].astype(f32)
    current = hidden[0].astype(f32) + norm_rows(branch, gains[1:2, :])
    current_b = current.astype(jnp.bfloat16)
    for j in range(members):
        fetch(j, mine).wait()
    gate = lax.dot_general(current_b, weights[0], (((1,), (1,)), ((), ())), preferred_element_type=f32)
    act = (gelu(gate) * (looked[...].astype(f32) * PLE**0.5)).astype(jnp.bfloat16)
    branch = jnp.dot(act, weights[1], preferred_element_type=f32)
    out[...] = (current + norm_rows(branch, gains[2:3, :])).astype(out.dtype)


def ple_chunk(me, keep, recv, from_x, from_y, hidden, gains, looked, mine, mate, order, chunk, count):
    width = hidden.shape[2]
    half, _, share, _ = mine.shape
    members = 2 * half
    block = pl.BlockSpec((1, count, width), lambda i, me: (0, 0, 0))
    flat = pl.BlockSpec((count, width), lambda i, me: (0, 0))
    anywhere = pl.BlockSpec(memory_space=pl.ANY)
    return pl.pallas_call(
        functools.partial(ple_body, order=order),
        out_shape=jax.ShapeDtypeStruct((count, width), jnp.bfloat16),
        grid_spec=pltpu.PrefetchScalarGridSpec(
            num_scalar_prefetch=1,
            grid=(1,),
            in_specs=[
                block,
                block,
                flat,
                flat,
                pl.BlockSpec((1, count, width), lambda i, me: (me[0], chunk, 0)),
                pl.BlockSpec(gains.shape, lambda i, me: (0, 0)),
                pl.BlockSpec((count, looked.shape[1]), lambda i, me: (chunk, 0)),
                anywhere,
                anywhere,
            ],
            out_specs=flat,
            scratch_shapes=[
                pltpu.VMEM((2, members * share, width), jnp.bfloat16),
                pltpu.SemaphoreType.DMA((members,)),
            ],
        ),
        compiler_params=pltpu.CompilerParams(dimension_semantics=("arbitrary",), vmem_limit_bytes=48 << 20),
        cost_estimate=pl.CostEstimate(flops=4 * count * width * members * share, bytes_accessed=members * share * width * 4, transcendentals=count * members * share),
        name="ple",
    )(me, keep, recv, from_x, from_y, hidden, gains, looked, mine, mate)


def far_body(keep, recv, low, high):
    total = (keep[0].astype(jnp.float32) + recv[0].astype(jnp.float32)).astype(low.dtype)
    low[...] = total[:, : low.shape[1]]
    high[...] = total[:, low.shape[1] :]


def far_sum(keep, recv):
    _, count, width = keep.shape
    block = pl.BlockSpec((1, count, width), lambda i: (3, 0, 0))
    part = pl.BlockSpec((count, width // 2), lambda i: (0, 0))
    out = jax.ShapeDtypeStruct((count, width // 2), keep.dtype)
    return pl.pallas_call(
        far_body,
        out_shape=(out, out),
        grid=(1,),
        in_specs=[block, block],
        out_specs=[part, part],
        cost_estimate=pl.CostEstimate(flops=count * width, bytes_accessed=6 * count * width, transcendentals=0),
        name="far",
    )(keep, recv)


def side_body(keep_x, recv_x, keep_y, recv_y, low, high, to_x, to_y):
    f32 = jnp.float32
    part = pl.program_id(0)
    x = keep_x[0].astype(f32) + recv_x[0].astype(f32)
    y = keep_y[0].astype(f32) + recv_y[0].astype(f32)

    @pl.when(part == 0)
    def _():
        to_x[...] = x.astype(to_x.dtype)
        to_y[...] = (y + low[...].astype(f32)).astype(to_y.dtype)

    @pl.when(part == 1)
    def _():
        to_x[...] = (x + high[...].astype(f32)).astype(to_x.dtype)
        to_y[...] = y.astype(to_y.dtype)


def side_sum(keep, recv, low, high):
    _, count, width = keep.shape
    half = width // 2
    block_x = pl.BlockSpec((1, count, half), lambda i: (1, 0, i))
    block_y = pl.BlockSpec((1, count, half), lambda i: (2, 0, i))
    part = pl.BlockSpec((count, half), lambda i: (0, 0))
    side = pl.BlockSpec((count, half), lambda i: (0, i))
    out = jax.ShapeDtypeStruct((count, width), keep.dtype)
    return pl.pallas_call(
        side_body,
        out_shape=(out, out),
        grid=(2,),
        in_specs=[block_x, block_x, block_y, block_y, part, part],
        out_specs=[side, side],
        compiler_params=pltpu.CompilerParams(dimension_semantics=("arbitrary",)),
        cost_estimate=pl.CostEstimate(flops=3 * count * width, bytes_accessed=14 * count * width, transcendentals=0),
        name="side",
    )(keep, recv, keep, recv, low, high)


def place_body(me, *refs, plan, count, aliased):
    n = len(plan)
    pieces = refs[:n]
    out = refs[n + aliased]
    stage, sems_in, sems_out = refs[n + aliased + 1 :]

    def take(i):
        size = plan[i][2]
        return pltpu.make_async_copy(pieces[i], stage.at[i, :, pl.ds(0, size)], sems_in.at[i])

    def put(i):
        relative, low, size, chunk = plan[i]
        return pltpu.make_async_copy(
            stage.at[i, :, pl.ds(0, size)],
            out.at[relative ^ me[0], pl.ds(chunk * count, count), pl.ds(low, size)],
            sems_out.at[i],
        )

    for i in range(n):
        take(i).start()
    for i in range(n):
        take(i).wait()
        put(i).start()
    for i in range(n):
        put(i).wait()


def place(me, pieces, out, shape, count):
    plan = [(r, low, a.shape[1], chunk) for r, low, a, chunk in pieces]
    arrays = [p[2] for p in pieces]
    aliased = out is not None
    anywhere = pl.BlockSpec(memory_space=pl.ANY)
    return pl.pallas_call(
        functools.partial(place_body, plan=plan, count=count, aliased=int(aliased)),
        out_shape=jax.ShapeDtypeStruct(shape, jnp.bfloat16),
        in_specs=[pl.BlockSpec(memory_space=pltpu.SMEM)] + [anywhere] * (len(arrays) + aliased),
        out_specs=anywhere,
        scratch_shapes=[
            pltpu.VMEM((len(arrays), count, shape[2]), jnp.bfloat16),
            pltpu.SemaphoreType.DMA((len(arrays),)),
            pltpu.SemaphoreType.DMA((len(arrays),)),
        ],
        input_output_aliases={1 + len(arrays): 0} if aliased else {},
        name="place",
    )(me, *arrays, *([out] if aliased else []))


def after(value, *others):
    return lax.optimization_barrier((value,) + others)[0]


def ask(token_slab, token_row, slab_owner, devices, slots):
    tokens = token_row.shape[0]
    hit_slab = token_slab == jnp.arange(slab_owner.shape[0], dtype=jnp.int32)[None, :]
    target = jnp.sum(jnp.where(hit_slab, slab_owner[None, :], 0), axis=1)
    order = jnp.arange(tokens, dtype=jnp.int32)
    earlier = (target[None, :] == target[:, None]) & (order[None, :] < order[:, None])
    slot_of = jnp.sum(earlier.astype(jnp.int32), axis=1)
    place_of = target * slots + slot_of
    hit = place_of[:, None] == jnp.arange(devices * slots, dtype=jnp.int32)[None, :]
    requests = jnp.sum(jnp.where(hit, token_row[:, None], 0), axis=0).reshape(devices, slots)
    return place_of, jnp.pad(requests, ((0, 0), (0, -slots % 128)))


def per_device(
    hidden,
    token_slab,
    token_row,
    slab_owner,
    ple_table,
    norm_gains,
    w_gate,
    w_up,
    w_down,
    ple_gate,
    ple_proj,
):
    members = lax.axis_size("member")
    axes = ("group", "member")
    devices = lax.axis_size("group") * members
    bits = members.bit_length() - 1
    bx, by = bits - 2, bits - 1
    near = list(range(bits - 2))
    width = hidden.shape[1]
    low = width // 2
    tokens = token_row.shape[0]
    count = tokens // CHUNKS
    channels = ple_table.shape[1]
    slots = max(2, (2 * tokens + devices - 1) // devices)
    slots += -slots % 16
    f32, bf16 = jnp.float32, jnp.bfloat16
    me = lax.axis_index("member").astype(jnp.int32)[None]
    blocks = hidden.reshape(members, tokens, width)
    gains = norm_gains[0]

    def swap(v, bit):
        return lax.ppermute(v, "member", [(i, i ^ (1 << bit)) for i in range(members)])

    def feed(chunk, *deps):
        return mlp_chunk(after(me, *deps), blocks, gains[0:1], w_gate[0], w_up[0], w_down[0], chunk, count)

    def reduce_near(keep, send):
        recv = swap(send, near[0])
        for bit in near[1:]:
            both = (keep.astype(f32) + recv.astype(f32)).astype(bf16)
            keep, send = both[: both.shape[0] // 2], both[both.shape[0] // 2 :]
            recv = swap(send, bit)
        return keep, recv

    def far_swap(parts):
        return swap(parts[0], bx), swap(parts[1], by)

    def side_swap(parts):
        return swap(parts[0], bx), swap(parts[1], by)

    order = [by, bx] + near
    small = [jnp.stack([ple_gate[0].T, ple_proj[0]])[None]]

    def spread(i):
        small.append(swap(small[i], order[i]))
        if i + 1 < len(order):
            small[i + 1] = jnp.concatenate(small[i : i + 2], axis=0)

    place_of, requests = ask(token_slab, token_row, slab_owner, devices, slots)
    wanted = lax.all_to_all(requests, axes, 0, 0, tiled=True)[:, :slots]

    spread(0)
    half = [feed(0, requests)]
    half.append(feed(1, half[0][0], small[1]))
    spread(1)
    summed = [reduce_near(*half[0])]
    far_out = far_sum(*summed[0])
    far = far_swap(far_out)
    summed.append(reduce_near(*half[1]))
    served = jnp.take(ple_table, after(wanted, *far_out).reshape(-1), axis=0, mode="clip")
    side_out = side_sum(*summed[0], after(far[0], served), far[1])
    side = [side_swap(side_out)]
    far_out = far_sum(*summed[1])
    returned = lax.all_to_all(
        after(served, *side_out, *far_out).reshape(devices, slots, channels), axes, 0, 0, tiled=True
    )
    far = far_swap(far_out)
    for i in range(2, len(order)):
        spread(i)
    side.append(side_swap(side_sum(*summed[1], *far)))
    hit = place_of[:, None] == jnp.arange(devices * slots, dtype=jnp.int32)[None, :]
    looked = jnp.dot(
        hit.astype(bf16), returned.reshape(devices * slots, channels), preferred_element_type=f32
    ).astype(bf16)

    x, y = 1 << bx, 1 << by
    pieces = []
    for chunk in range(CHUNKS):
        own = ple_chunk(me, *summed[chunk], *side[chunk], blocks, gains, looked, *small[-2:], order, chunk, count)
        x_own = swap(own, bx)
        y_own = swap(own, by)
        early = [(0, 0, own), (x, 0, x_own), (y, 0, y_own)]
        late = [(x | y, 0, swap(y_own[:, :low], bx)), (x | y, low, swap(x_own[:, low:], by))]
        for group in (early, late):
            for bit in reversed(near):
                group = group + [(r | (1 << bit), start, swap(a, bit)) for r, start, a in group]
            pieces.append([p + (chunk,) for p in group])
    out = None
    for group in (pieces[0], pieces[1] + pieces[2], pieces[3]):
        out = place(me, group, out, blocks.shape, count)
    return out.reshape(hidden.shape)


def solution(mesh):
    return jax.shard_map(
        per_device,
        mesh=mesh,
        in_specs=(
            P("group", None),
            P(("group", "member"), None),
            P(("group", "member")),
            P(),
            P(("group", "member"), None),
            P(),
            P(None, None, "member"),
            P(None, None, "member"),
            P(None, "member", None),
            P(None, None, "member"),
            P(None, "member", None),
        ),
        out_specs=P("group", None),
        check_vma=False,
    )
```

time: 418 us -> 150 us (0.36)
  waiting for transfers between devices: 227 us -> 38.9 us
  blocking collectives: 72.4 us -> 11.9 us
  Pallas kernels: 0 us -> 55.5 us
  matrix products: 50.5 us -> 1.2 us
  other arithmetic: 44 us -> 2.94 us
  starting transfers between devices: 0.31 us -> 26.2 us
  between operations: 13.4 us -> 0.5 us
    reduce_scatter x2 -> x0, waiting for transfers between devices: 178 us -> none  [combine_branch(): lax.psum_scatter(partial_value, 'member', scatter_dimension=1, tiled=True)]
    pallas_call x0 -> x11, Pallas kernels: none -> 55.5 us  [the longest x2 31.1 us: mlp_chunk(): pl.pallas_call(functools.partial(mlp_body, order=order, first=chunk * cou...]
    dot_general x5 -> x1, matrix products: 50.5 us -> 1.2 us  [per_device(): jnp.dot(hit.astype(bf16), returned.reshape(devices * slots, channels), pr...]
    all_gather x2 -> x0, waiting for transfers between devices: 49.1 us -> none  [combine_branch(): return lax.all_gather(updated, 'member', axis=1, tiled=True)]
    ppermute x0 -> x31, waiting for transfers between devices: none -> 38.9 us  [swap(): lax.ppermute(v, 'member', [(i, i ^ 1 << bit) for i in range(members)])]
    all_to_all x5 -> x1, blocking collectives: 46.9 us -> 11.9 us  [per_device(): wanted = lax.all_to_all(requests, axes, 0, 0, tiled=True)[:, :slots]]
    psum x2 -> x0, blocking collectives: 25.5 us -> none  [combine_branch(): squares = lax.psum(jnp.sum(share * share, axis=-1, keepdims=True), 'member')]
    ppermute x0 -> x31, starting transfers between devices: none -> 22.7 us  [swap(): lax.ppermute(v, 'member', [(i, i ^ 1 << bit) for i in range(members)])]
  transfers between devices with their start and end apart: 4 -> 32, of which waited for: 4 -> 15; matrix products, arithmetic and copies ran while one was open for 9% -> 6% of each run, Pallas kernels for 0% -> 36%
where the time goes in v1:
time: 150 us
  Pallas kernels  55.5 us (37%)
  waiting for transfers between devices  38.9 us (26%)
  starting transfers between devices  26.2 us (17%)
  local copies, waits for them, and re-layouts  12.6 us (8%)
  blocking collectives  11.9 us (8%)
  other arithmetic  2.94 us (2%)
    ppermute x31, waiting for transfers between devices, swap(): lax.ppermute(v, 'member', [(i, i ^ 1 << bit) for i in range(members)])  38.9 us
    pallas_call x2, Pallas kernels, mlp_chunk(): pl.pallas_call(functools.partial(mlp_body, order=order, first=chunk * cou...  31.1 us
    ppermute x31, starting transfers between devices, swap(): lax.ppermute(v, 'member', [(i, i ^ 1 << bit) for i in range(members)])  22.7 us
    all_to_all x1, blocking collectives, per_device(): wanted = lax.all_to_all(requests, axes, 0, 0, tiled=True)[:, :slots]  11.9 us
    pallas_call x2, Pallas kernels, ple_chunk(): pl.pallas_call(functools.partial(ple_body, order=order), out_shape=jax.Sh...  7.72 us
    pallas_call x3, Pallas kernels, place(): pl.pallas_call(functools.partial(place_body, plan=plan, count=count, alia...  7.61 us
    unnamed x47, local copies, waits for them, and re-layouts  6.78 us
    pallas_call x2, Pallas kernels, side_sum(): pl.pallas_call(side_body, out_shape=(out, out), grid=(2,), in_specs=[bloc...  5.25 us
  transfers between devices with their start and end apart: 32, of which 15 were waited for; matrix products, arithmetic and copies ran while one was open for 6% of the time, Pallas kernels for 36%

profile of v1, /device:TPU:0, one launch (start us, length us, event | category | flops | bytes accessed | tf_op | source)
XLA Modules:
  0.0 149.8 jit_solution(11846752205635403622)
XLA Ops:
  1.0 3.1 %collective-permute-start = (bf16[1,2,32,2048]{3,2,1,0:T(8,128)(2,1)S(1)}, bf16[1,2,32,2048]{3,2,1,0:T(8,128)(2,1)S(1)}, u32[]{:S(2)}, u32[]{:S(2)}) collective-permute-start(bf16[1,2,32,2048]{3,2,1,0:T(8,128)(2,1)S(1)} %maximum_bitcast_fusion), channel_id=1, source_target_pairs={{0,4},{1,5},{2,6},{3,7},{4,0},{5,1},{6,2},{7,3},{8,12},{9,13},{10,... | collective-permute-start | bytes 786440 | tf_op jit(solution)/shard_map/ppermute | solution.py:364
  6.6 15.7 %mlp.2 = (bf16[4,96,2048]{2,1,0:T(8,128)(2,1)S(1)}, bf16[4,96,2048]{2,1,0:T(8,128)(2,1)S(1)}) custom-call(s32[1]{0:T(128)} %bitcast.me, bf16[8,192,2048]{2,1,0:T(8,128)(2,1)} %bitcast.29, f32[1,2048]{1,0:T(1,128)S(1)} %slice_bitcast_fusion.gains, bf16[2048,1024]{1,0:T(8,128)(2,1)} %bitcast.37, bf16[2048,1024]{1,0:T(8,128)(2,1)} %bitcast.39, ...), custom_call_target="tpu_custom_call" | custom-call | flops 9663676416 | bytes 12582912 | tf_op jit(solution)/shard_map/mlp/pallas_call | solution.py:111
  23.6 15.4 %mlp.3 = (bf16[4,96,2048]{2,1,0:T(8,128)(2,1)S(1)}, bf16[4,96,2048]{2,1,0:T(8,128)(2,1)S(1)}) custom-call(s32[1]{0:T(128)} %bitcast.me, bf16[8,192,2048]{2,1,0:T(8,128)(2,1)} %bitcast.30, f32[1,2048]{1,0:T(1,128)S(1)} %slice_bitcast_fusion.gains, bf16[2048,1024]{1,0:T(8,128)(2,1)} %bitcast.38, bf16[2048,1024]{1,0:T(8,128)(2,1)} %bitcast.40, ...), custom_call_target="tpu_custom_call" | custom-call | flops 9663676416 | bytes 12582912 | tf_op jit(solution)/shard_map/mlp/pallas_call | solution.py:111
  40.6 1.5 collective-permute-start.9
  42.1 12.3 %collective-permute-done.9 = bf16[2,2,32,2048]{3,2,1,0:T(8,128)(2,1)S(1)} collective-permute-done((bf16[2,2,32,2048]{3,2,1,0:T(8,128)(2,1)S(1)}, bf16[2,2,32,2048]{3,2,1,0:T(8,128)(2,1)S(1)}, u32[]{:S(2)}, u32[]{:S(2)}) %collective-permute-start.9) | collective-permute-done | bytes 524320 | tf_op jit(solution)/shard_map/ppermute | solution.py:364
  54.7 1.9 %far.3 = (bf16[96,1024]{1,0:T(8,128)(2,1)}, bf16[96,1024]{1,0:T(8,128)(2,1)}) custom-call(bf16[4,96,2048]{2,1,0:T(8,128)(2,1)} %copy-done.2, bf16[4,96,2048]{2,1,0:T(8,128)(2,1)} %collective-permute-done.6.recv.recv_x.recv_y), custom_call_target="tpu_custom_call" | custom-call | flops 196608 | bytes 1179648 | tf_op jit(solution)/shard_map/far/pallas_call | solution.py:220
  58.6 11.9 %all_to_all.17 = s32[32,1,128]{2,1,0:T(1,128)S(1)} all-to-all(s32[32,1,128]{2,1,0:T(1,128)S(1)} %bitcast.34), channel_id=1, replica_groups=mesh['group'=4,'member'=8] {'group','member'}, dimensions={0} | all-to-all | bytes 32768 | tf_op jit(solution)/shard_map/all_to_all | solution.py:392
  70.6 4.9 %gather_fusion = bf16[512,256]{1,0:T(8,128)(2,1)} fusion(bf16[8192,256]{1,0:T(8,128)(2,1)} %param.15, s32[1024]{0:T(1024)S(1)} %pad_clamp_fusion), kind=kCustom, calls=%fused_computation | custom fusion | bytes 526336 | tf_op jit(solution)/shard_map/jit(_take)/gather | solution.py:402
  76.8 2.6 %side.3 = (bf16[96,2048]{1,0:T(8,128)(2,1)}, bf16[96,2048]{1,0:T(8,128)(2,1)}) custom-call(bf16[4,96,2048]{2,1,0:T(8,128)(2,1)} %copy-done.2, bf16[4,96,2048]{2,1,0:T(8,128)(2,1)} %collective-permute-done.6.recv.recv_x.recv_y, bf16[4,96,2048]{2,1,0:T(8,128)(2,1)} %copy-done.2, bf16[4,96,2048]{2,1,0:T(8,128)(2,1)} %collective-permute-done.6.recv.recv_x.recv_y, ...), custom_call_target="tpu_custom_call" | custom-call | flops 589824 | bytes 2752512 | tf_op jit(solution)/shard_map/side/pallas_call | solution.py:256
  79.4 1.9 %far.2 = (bf16[96,1024]{1,0:T(8,128)(2,1)}, bf16[96,1024]{1,0:T(8,128)(2,1)}) custom-call(bf16[4,96,2048]{2,1,0:T(8,128)(2,1)} %copy-done, bf16[4,96,2048]{2,1,0:T(8,128)(2,1)} %collective-permute-done.1.recv.recv_x.recv_y), custom_call_target="tpu_custom_call" | custom-call | flops 196608 | bytes 1179648 | tf_op jit(solution)/shard_map/far/pallas_call | solution.py:220
  81.4 3.4 %all-to-all-start.1 = ((bf16[32,16,256]{2,1,0:T(8,128)(2,1)}), bf16[32,16,256]{2,1,0:T(8,128)(2,1)}, u32[]{:S(2)}, u32[]{:S(2)}) async-start(bf16[32,16,256]{2,1,0:T(8,128)(2,1)} %bitcast.14), calls=%async_computation.1 | async-start | bytes 524288 | tf_op jit(solution)/shard_map/all_to_all | solution.py:406
  84.8 1.6 %collective-permute-start.2 = (bf16[96,1024]{1,0:T(8,128)(2,1)}, bf16[96,1024]{1,0:T(8,128)(2,1)S(1)}, u32[]{:S(2)}, u32[]{:S(2)}) collective-permute-start(bf16[96,1024]{1,0:T(8,128)(2,1)} %get-tuple-element.27), channel_id=1, source_target_pairs={{0,2},{1,3},{2,0},{3,1},{4,6},{5,7},{6,4},{7,5},{8,10},{9,11},{10,... | collective-permute-start | bytes 589832 | tf_op jit(solution)/shard_map/ppermute | solution.py:364
  86.4 1.5 collective-permute-start.3
  88.9 6.0 %collective-permute-done.2.low = bf16[96,1024]{1,0:T(8,128)(2,1)S(1)} collective-permute-done((bf16[96,1024]{1,0:T(8,128)(2,1)}, bf16[96,1024]{1,0:T(8,128)(2,1)S(1)}, u32[]{:S(2)}, u32[]{:S(2)}) %collective-permute-start.2) | collective-permute-done | bytes 196640 | tf_op jit(solution)/shard_map/ppermute | solution.py:364
  96.4 2.6 %side.2 = (bf16[96,2048]{1,0:T(8,128)(2,1)}, bf16[96,2048]{1,0:T(8,128)(2,1)}) custom-call(bf16[4,96,2048]{2,1,0:T(8,128)(2,1)} %copy-done, bf16[4,96,2048]{2,1,0:T(8,128)(2,1)} %collective-permute-done.1.recv.recv_x.recv_y, bf16[4,96,2048]{2,1,0:T(8,128)(2,1)} %copy-done, bf16[4,96,2048]{2,1,0:T(8,128)(2,1)} %collective-permute-done.1.recv.recv_x.recv_y, ...), custom_call_target="tpu_custom_call" | custom-call | flops 589824 | bytes 2752512 | tf_op jit(solution)/shard_map/side/pallas_call | solution.py:256
  105.3 3.9 %ple.3.refs_0_ = bf16[96,2048]{1,0:T(8,128)(2,1)S(1)} custom-call(s32[1]{0:T(128)} %bitcast.me, bf16[4,96,2048]{2,1,0:T(8,128)(2,1)S(1)} %copy-done.3, bf16[4,96,2048]{2,1,0:T(8,128)(2,1)} %collective-permute-done.6.recv.recv_x.recv_y, bf16[96,2048]{1,0:T(8,128)(2,1)S(1)} %copy-done.7, bf16[96,2048]{1,0:T(8,128)(2,1)} %collective-permute-done.18.from_y, ...), custom_call_target="tpu_custom_call" | custom-call | flops 201326592 | bytes 2097152 | tf_op jit(solution)/shard_map/ple/pallas_call | solution.py:180
  112.7 3.8 %ple.2.refs_4_ = bf16[96,2048]{1,0:T(8,128)(2,1)S(1)} custom-call(s32[1]{0:T(128)} %bitcast.me, bf16[4,96,2048]{2,1,0:T(8,128)(2,1)S(1)} %copy-done.1, bf16[4,96,2048]{2,1,0:T(8,128)(2,1)} %collective-permute-done.1.recv.recv_x.recv_y, bf16[96,2048]{1,0:T(8,128)(2,1)S(1)} %collective-permute-done.4.from_x, bf16[96,2048]{1,0:T(8,128)(2,1)} %collective-permute-done.5.from_y, ...), custom_call_target="tpu_custom_call" | custom-call | flops 201326592 | bytes 2097152 | tf_op jit(solution)/shard_map/ple/pallas_call | solution.py:180
  118.3 3.0 %collective-permute-done.19.refs_2_ = bf16[96,2048]{1,0:T(8,128)(2,1)S(1)} collective-permute-done((bf16[96,2048]{1,0:T(8,128)(2,1)S(1)}, bf16[96,2048]{1,0:T(8,128)(2,1)S(1)}, u32[]{:S(2)}, u32[]{:S(2)}) %collective-permute-start.19) | collective-permute-done | bytes 393248 | tf_op jit(solution)/shard_map/ppermute | solution.py:364
  123.5 5.5 %collective-permute-done.11.refs_6_ = bf16[96,2048]{1,0:T(8,128)(2,1)S(1)} collective-permute-done((bf16[96,2048]{1,0:T(8,128)(2,1)S(1)}, bf16[96,2048]{1,0:T(8,128)(2,1)S(1)}, u32[]{:S(2)}, u32[]{:S(2)}) %collective-permute-start.11) | collective-permute-done | bytes 393248 | tf_op jit(solution)/shard_map/ppermute | solution.py:364
  134.0 1.8 %collective-permute-done.22.refs_1_ = bf16[96,1024]{1,0:T(8,128)(2,1)} collective-permute-done((bf16[96,1024]{1,0:T(8,128)(2,1)S(1)}, bf16[96,1024]{1,0:T(8,128)(2,1)}, u32[]{:S(2)}, u32[]{:S(2)}) %collective-permute-start.22) | collective-permute-done | bytes 196640 | tf_op jit(solution)/shard_map/ppermute | solution.py:364
  135.7 2.8 %collective-permute-done.12.refs_0_ = bf16[96,1024]{1,0:T(8,128)(2,1)} collective-permute-done((bf16[96,1024]{1,0:T(8,128)(2,1)S(1)}, bf16[96,1024]{1,0:T(8,128)(2,1)}, u32[]{:S(2)}, u32[]{:S(2)}) %collective-permute-start.12) | collective-permute-done | bytes 196640 | tf_op jit(solution)/shard_map/ppermute | solution.py:364
  141.9 2.5 %place.3.refs_10_ = bf16[8,192,2048]{2,1,0:T(8,128)(2,1)} custom-call(s32[1]{0:T(128)} %bitcast.me, bf16[96,2048]{1,0:T(8,128)(2,1)} %copy-done.4, bf16[96,2048]{1,0:T(8,128)(2,1)} %copy-done.9, bf16[96,2048]{1,0:T(8,128)(2,1)} %copy-done.8, bf16[96,2048]{1,0:T(8,128)(2,1)} %copy-done.12, bf16[96,2048]{1,0:T(8,128)(2,1)} %copy-done.13, ...), custom_call_target="tpu_custom_call" | custom-call | tf_op jit(solution)/shard_map/place/pallas_call | solution.py:300
  144.4 3.1 %place.4.refs_4_ = bf16[8,192,2048]{2,1,0:T(8,128)(2,1)} custom-call(s32[1]{0:T(128)} %bitcast.me, bf16[96,1024]{1,0:T(8,128)(2,1)} %copy-done.16, bf16[96,1024]{1,0:T(8,128)(2,1)} %collective-permute-done.22.refs_1_, bf16[96,1024]{1,0:T(8,128)(2,1)} %copy-done.17, ...), custom_call_target="tpu_custom_call", output_to_operand_aliasing={{}: (11, {})} | custom-call | tf_op jit(solution)/shard_map/place/pallas_call | solution.py:300
  147.6 2.0 %place.5 = bf16[8,192,2048]{2,1,0:T(8,128)(2,1)} custom-call(s32[1]{0:T(128)} %bitcast.me, bf16[96,1024]{1,0:T(8,128)(2,1)} %collective-permute-done.12.refs_0_, bf16[96,1024]{1,0:T(8,128)(2,1)} %collective-permute-done.14.refs_1_, bf16[96,1024]{1,0:T(8,128)(2,1)} %collective-permute-done.15.refs_2_, ...), custom_call_target="tpu_custom_call", output_to_operand_aliasing={{}: (5, {})} | custom-call | tf_op jit(solution)/shard_map/place/pallas_call | solution.py:300
  (117 shorter events, 34.3 us)
Async XLA Ops:
  1.0 22.5 %collective-permute-start = (bf16[1,2,32,2048]{3,2,1,0:T(8,128)(2,1)S(1)}, bf16[1,2,32,2048]{3,2,1,0:T(8,128)(2,1)S(1)}, u32[]{:S(2)}, u32[]{:S(2)}) collective-permute-start(bf16[1,2,32,2048]{3,2,1,0:T(8,128)(2,1)S(1)} %maximum_bitcast_fusion), channel_id=1, source_target_pairs={{0,4},{1,5},{2,6},{3,7},{4,0},{5,1},{6,2},{7,3},{8,12},{9,13},{10,... | collective-permute-start | bytes 786440 | tf_op jit(solution)/shard_map/ppermute | solution.py:364
  23.5 31.1 %collective-permute-start.6 = (bf16[4,96,2048]{2,1,0:T(8,128)(2,1)S(1)}, bf16[4,96,2048]{2,1,0:T(8,128)(2,1)}, u32[]{:S(2)}, u32[]{:S(2)}) collective-permute-start(bf16[4,96,2048]{2,1,0:T(8,128)(2,1)S(1)} %get-tuple-element.31), channel_id=1, source_target_pairs={{0,1},{1,0},{2,3},{3,2},{4,5},{5,4},{6,7},{7,6},{8,9},{9,8},{10,11... | collective-permute-start | bytes 4718600 | tf_op jit(solution)/shard_map/ppermute | solution.py:364
  40.1 39.3 %collective-permute-start.1 = (bf16[4,96,2048]{2,1,0:T(8,128)(2,1)S(1)}, bf16[4,96,2048]{2,1,0:T(8,128)(2,1)}, u32[]{:S(2)}, u32[]{:S(2)}) collective-permute-start(bf16[4,96,2048]{2,1,0:T(8,128)(2,1)S(1)} %get-tuple-element.26), channel_id=1, source_target_pairs={{0,1},{1,0},{2,3},{3,2},{4,5},{5,4},{6,7},{7,6},{8,9},{9,8},{10,11... | collective-permute-start | bytes 4718600 | tf_op jit(solution)/shard_map/ppermute | solution.py:364
  40.6 13.8 %collective-permute-start.9 = (bf16[2,2,32,2048]{3,2,1,0:T(8,128)(2,1)S(1)}, bf16[2,2,32,2048]{3,2,1,0:T(8,128)(2,1)S(1)}, u32[]{:S(2)}, u32[]{:S(2)}) collective-permute-start(bf16[2,2,32,2048]{3,2,1,0:T(8,128)(2,1)S(1)} %pad_maximum_fusion.1), channel_id=1, source_target_pairs={{0,2},{1,3},{2,0},{3,1},{4,6},{5,7},{6,4},{7,5},{8,10},{9,11},{10,... | collective-permute-start | bytes 1572872 | tf_op jit(solution)/shard_map/ppermute | solution.py:364
  54.6 48.1 %collective-permute-start.10 = (bf16[4,2,32,2048]{3,2,1,0:T(8,128)(2,1)S(1)}, bf16[4,2,32,2048]{3,2,1,0:T(8,128)(2,1)}, u32[]{:S(2)}, u32[]{:S(2)}) collective-permute-start(bf16[4,2,32,2048]{3,2,1,0:T(8,128)(2,1)S(1)} %pad_maximum_fusion.mine), channel_id=1, source_target_pairs={{0,1},{1,0},{2,3},{3,2},{4,5},{5,4},{6,7},{7,6},{8,9},{9,8},{10,11... | collective-permute-start | bytes 3145736 | tf_op jit(solution)/shard_map/ppermute | solution.py:364
  56.6 18.9 %collective-permute-start.7 = (bf16[96,1024]{1,0:T(8,128)(2,1)}, bf16[96,1024]{1,0:T(8,128)(2,1)S(1)}, u32[]{:S(2)}, u32[]{:S(2)}) collective-permute-start(bf16[96,1024]{1,0:T(8,128)(2,1)} %get-tuple-element.32), channel_id=1, source_target_pairs={{0,2},{1,3},{2,0},{3,1},{4,6},{5,7},{6,4},{7,5},{8,10},{9,11},{10,... | collective-permute-start | bytes 589832 | tf_op jit(solution)/shard_map/ppermute | solution.py:364
  58.1 17.4 %collective-permute-start.8 = (bf16[96,1024]{1,0:T(8,128)(2,1)}, bf16[96,1024]{1,0:T(8,128)(2,1)S(1)}, u32[]{:S(2)}, u32[]{:S(2)}) collective-permute-start(bf16[96,1024]{1,0:T(8,128)(2,1)} %get-tuple-element.33), channel_id=1, source_target_pairs={{0,4},{1,5},{2,6},{3,7},{4,0},{5,1},{6,2},{7,3},{8,12},{9,13},{10,... | collective-permute-start | bytes 589832 | tf_op jit(solution)/shard_map/ppermute | solution.py:364
  81.4 20.1 %all-to-all-start.1 = ((bf16[32,16,256]{2,1,0:T(8,128)(2,1)}), bf16[32,16,256]{2,1,0:T(8,128)(2,1)}, u32[]{:S(2)}, u32[]{:S(2)}) async-start(bf16[32,16,256]{2,1,0:T(8,128)(2,1)} %bitcast.14), calls=%async_computation.1 | async-start | bytes 524288 | tf_op jit(solution)/shard_map/all_to_all | solution.py:406
  84.8 10.2 %collective-permute-start.2 = (bf16[96,1024]{1,0:T(8,128)(2,1)}, bf16[96,1024]{1,0:T(8,128)(2,1)S(1)}, u32[]{:S(2)}, u32[]{:S(2)}) collective-permute-start(bf16[96,1024]{1,0:T(8,128)(2,1)} %get-tuple-element.27), channel_id=1, source_target_pairs={{0,2},{1,3},{2,0},{3,1},{4,6},{5,7},{6,4},{7,5},{8,10},{9,11},{10,... | collective-permute-start | bytes 589832 | tf_op jit(solution)/shard_map/ppermute | solution.py:364
  86.4 9.3 %collective-permute-start.3 = (bf16[96,1024]{1,0:T(8,128)(2,1)}, bf16[96,1024]{1,0:T(8,128)(2,1)S(1)}, u32[]{:S(2)}, u32[]{:S(2)}) collective-permute-start(bf16[96,1024]{1,0:T(8,128)(2,1)} %get-tuple-element.28), channel_id=1, source_target_pairs={{0,4},{1,5},{2,6},{3,7},{4,0},{5,1},{6,2},{7,3},{8,12},{9,13},{10,... | collective-permute-start | bytes 589832 | tf_op jit(solution)/shard_map/ppermute | solution.py:364
  87.9 15.5 %collective-permute-start.17 = (bf16[96,2048]{1,0:T(8,128)(2,1)}, bf16[96,2048]{1,0:T(8,128)(2,1)S(1)}, u32[]{:S(2)}, u32[]{:S(2)}) collective-permute-start(bf16[96,2048]{1,0:T(8,128)(2,1)} %get-tuple-element.36), channel_id=1, source_target_pairs={{0,2},{1,3},{2,0},{3,1},{4,6},{5,7},{6,4},{7,5},{8,10},{9,11},{10,... | collective-permute-start | bytes 1179656 | tf_op jit(solution)/shard_map/ppermute | solution.py:364
  88.5 15.8 %collective-permute-start.18 = (bf16[96,2048]{1,0:T(8,128)(2,1)}, bf16[96,2048]{1,0:T(8,128)(2,1)}, u32[]{:S(2)}, u32[]{:S(2)}) collective-permute-start(bf16[96,2048]{1,0:T(8,128)(2,1)} %get-tuple-element.37), channel_id=1, source_target_pairs={{0,4},{1,5},{2,6},{3,7},{4,0},{5,1},{6,2},{7,3},{8,12},{9,13},{10,... | collective-permute-start | bytes 1179656 | tf_op jit(solution)/shard_map/ppermute | solution.py:364
  99.1 12.6 %collective-permute-start.4 = (bf16[96,2048]{1,0:T(8,128)(2,1)}, bf16[96,2048]{1,0:T(8,128)(2,1)S(1)}, u32[]{:S(2)}, u32[]{:S(2)}) collective-permute-start(bf16[96,2048]{1,0:T(8,128)(2,1)} %get-tuple-element.29), channel_id=1, source_target_pairs={{0,2},{1,3},{2,0},{3,1},{4,6},{5,7},{6,4},{7,5},{8,10},{9,11},{10,... | collective-permute-start | bytes 1179656 | tf_op jit(solution)/shard_map/ppermute | solution.py:364
  100.0 12.7 %collective-permute-start.5 = (bf16[96,2048]{1,0:T(8,128)(2,1)}, bf16[96,2048]{1,0:T(8,128)(2,1)}, u32[]{:S(2)}, u32[]{:S(2)}) collective-permute-start(bf16[96,2048]{1,0:T(8,128)(2,1)} %get-tuple-element.30), channel_id=1, source_target_pairs={{0,4},{1,5},{2,6},{3,7},{4,0},{5,1},{6,2},{7,3},{8,12},{9,13},{10,... | collective-permute-start | bytes 1179656 | tf_op jit(solution)/shard_map/ppermute | solution.py:364
  109.2 12.1 %collective-permute-start.19 = (bf16[96,2048]{1,0:T(8,128)(2,1)S(1)}, bf16[96,2048]{1,0:T(8,128)(2,1)S(1)}, u32[]{:S(2)}, u32[]{:S(2)}) collective-permute-start(bf16[96,2048]{1,0:T(8,128)(2,1)S(1)} %ple.3.refs_0_), channel_id=1, source_target_pairs={{0,4},{1,5},{2,6},{3,7},{4,0},{5,1},{6,2},{7,3},{8,12},{9,13},{10,... | collective-permute-start | bytes 1179656 | tf_op jit(solution)/shard_map/ppermute | solution.py:364
  110.7 11.8 %collective-permute-start.21 = (bf16[96,2048]{1,0:T(8,128)(2,1)S(1)}, bf16[96,2048]{1,0:T(8,128)(2,1)S(1)}, u32[]{:S(2)}, u32[]{:S(2)}) collective-permute-start(bf16[96,2048]{1,0:T(8,128)(2,1)S(1)} %ple.3.refs_0_), channel_id=1, source_target_pairs={{0,2},{1,3},{2,0},{3,1},{4,6},{5,7},{6,4},{7,5},{8,10},{9,11},{10,... | collective-permute-start | bytes 1179656 | tf_op jit(solution)/shard_map/ppermute | solution.py:364
  116.5 12.5 %collective-permute-start.11 = (bf16[96,2048]{1,0:T(8,128)(2,1)S(1)}, bf16[96,2048]{1,0:T(8,128)(2,1)S(1)}, u32[]{:S(2)}, u32[]{:S(2)}) collective-permute-start(bf16[96,2048]{1,0:T(8,128)(2,1)S(1)} %ple.2.refs_4_), channel_id=1, source_target_pairs={{0,4},{1,5},{2,6},{3,7},{4,0},{5,1},{6,2},{7,3},{8,12},{9,13},{10,... | collective-permute-start | bytes 1179656 | tf_op jit(solution)/shard_map/ppermute | solution.py:364
  117.8 13.1 %collective-permute-start.13 = (bf16[96,2048]{1,0:T(8,128)(2,1)S(1)}, bf16[96,2048]{1,0:T(8,128)(2,1)S(1)}, u32[]{:S(2)}, u32[]{:S(2)}) collective-permute-start(bf16[96,2048]{1,0:T(8,128)(2,1)S(1)} %ple.2.refs_4_), channel_id=1, source_target_pairs={{0,2},{1,3},{2,0},{3,1},{4,6},{5,7},{6,4},{7,5},{8,10},{9,11},{10,... | collective-permute-start | bytes 1179656 | tf_op jit(solution)/shard_map/ppermute | solution.py:364
  118.3 12.7 %collective-permute-start.28 = (bf16[96,2048]{1,0:T(8,128)(2,1)S(1)}, bf16[96,2048]{1,0:T(8,128)(2,1)S(1)}, u32[]{:S(2)}, u32[]{:S(2)}) collective-permute-start(bf16[96,2048]{1,0:T(8,128)(2,1)S(1)} %ple.3.refs_0_), channel_id=1, source_target_pairs={{0,1},{1,0},{2,3},{3,2},{4,5},{5,4},{6,7},{7,6},{8,9},{9,8},{10,11... | collective-permute-start | bytes 1179656 | tf_op jit(solution)/shard_map/ppermute | solution.py:364
  121.3 10.3 %collective-permute-start.25 = (bf16[96,2048]{1,0:T(8,128)(2,1)S(1)}, bf16[96,2048]{1,0:T(8,128)(2,1)S(1)}, u32[]{:S(2)}, u32[]{:S(2)}) collective-permute-start(bf16[96,2048]{1,0:T(8,128)(2,1)S(1)} %ple.2.refs_4_), channel_id=1, source_target_pairs={{0,1},{1,0},{2,3},{3,2},{4,5},{5,4},{6,7},{7,6},{8,9},{9,8},{10,11... | collective-permute-start | bytes 1179656 | tf_op jit(solution)/shard_map/ppermute | solution.py:364
  122.5 10.8 %collective-permute-start.20 = (bf16[96,1024]{1,0:T(8,128)(2,1)S(1)}, bf16[96,1024]{1,0:T(8,128)(2,1)S(1)}, u32[]{:S(2)}, u32[]{:S(2)}) collective-permute-start(bf16[96,1024]{1,0:T(8,128)(2,1)S(1)} %slice.34), channel_id=1, source_target_pairs={{0,2},{1,3},{2,0},{3,1},{4,6},{5,7},{6,4},{7,5},{8,10},{9,11},{10,... | collective-permute-start | bytes 589832 | tf_op jit(solution)/shard_map/ppermute | solution.py:364
  130.9 8.7 %collective-permute-start.29 = (bf16[96,2048]{1,0:T(8,128)(2,1)S(1)}, bf16[96,2048]{1,0:T(8,128)(2,1)S(1)}, u32[]{:S(2)}, u32[]{:S(2)}) collective-permute-start(bf16[96,2048]{1,0:T(8,128)(2,1)S(1)} %collective-permute-done.21.refs_1_), channel_id=1, source_target_pairs={{0,1},{1,0},{2,3},{3,2},{4,5},{5,4},{6,7},{7,6},{8,9},{9,8},{10,11... | collective-permute-start | bytes 1179656 | tf_op jit(solution)/shard_map/ppermute | solution.py:364
  131.0 9.1 %collective-permute-start.30 = (bf16[96,2048]{1,0:T(8,128)(2,1)S(1)}, bf16[96,2048]{1,0:T(8,128)(2,1)S(1)}, u32[]{:S(2)}, u32[]{:S(2)}) collective-permute-start(bf16[96,2048]{1,0:T(8,128)(2,1)S(1)} %collective-permute-done.19.refs_2_), channel_id=1, source_target_pairs={{0,1},{1,0},{2,3},{3,2},{4,5},{5,4},{6,7},{7,6},{8,9},{9,8},{10,11... | collective-permute-start | bytes 1179656 | tf_op jit(solution)/shard_map/ppermute | solution.py:364
  135.7 8.7 %collective-permute-start.26 = (bf16[96,2048]{1,0:T(8,128)(2,1)S(1)}, bf16[96,2048]{1,0:T(8,128)(2,1)}, u32[]{:S(2)}, u32[]{:S(2)}) collective-permute-start(bf16[96,2048]{1,0:T(8,128)(2,1)S(1)} %collective-permute-done.13.refs_5_), channel_id=1, source_target_pairs={{0,1},{1,0},{2,3},{3,2},{4,5},{5,4},{6,7},{7,6},{8,9},{9,8},{10,11... | collective-permute-start | bytes 1179656 | tf_op jit(solution)/shard_map/ppermute | solution.py:364
  (31 other events, 239.7 us)

commit v2 on v1

--- a/solution.py
+++ b/solution.py
@@ -112,7 +112,7 @@
         functools.partial(mlp_body, order=order, first=chunk * count, count=count, parts=parts),
         out_shape=(out, out),
         in_specs=[pl.BlockSpec(memory_space=pltpu.SMEM), anywhere, pl.BlockSpec(memory_space=pltpu.VMEM)] + [anywhere] * 3,
-        out_specs=[anywhere, anywhere],
+        out_specs=[pl.BlockSpec(memory_space=pltpu.HBM)] * 2,
         scratch_shapes=[
             pltpu.VMEM((members, count, width), jnp.bfloat16),
             pltpu.VMEM((tiles, width, tile), jnp.bfloat16),
@@ -393,23 +393,16 @@
 
     spread(0)
     half = [feed(0, requests)]
-    half.append(feed(1, half[0][0], small[1]))
+    served = jnp.take(ple_table, after(wanted, half[0][0]).reshape(-1), axis=0, mode="clip")
+    returned = lax.all_to_all(served.reshape(devices, slots, channels), axes, 0, 0, tiled=True)
+    half.append(feed(1, half[0][0], small[1], served))
     spread(1)
-    summed = [reduce_near(*half[0])]
-    far_out = far_sum(*summed[0])
-    far = far_swap(far_out)
-    summed.append(reduce_near(*half[1]))
-    served = jnp.take(ple_table, after(wanted, *far_out).reshape(-1), axis=0, mode="clip")
-    side_out = side_sum(*summed[0], after(far[0], served), far[1])
-    side = [side_swap(side_out)]
-    far_out = far_sum(*summed[1])
-    returned = lax.all_to_all(
-        after(served, *side_out, *far_out).reshape(devices, slots, channels), axes, 0, 0, tiled=True
-    )
-    far = far_swap(far_out)
+    summed = [reduce_near(*half[chunk]) for chunk in range(CHUNKS)]
+    far_out = [far_sum(*summed[chunk]) for chunk in range(CHUNKS)]
+    far = [far_swap(far_out[chunk]) for chunk in range(CHUNKS)]
     for i in range(2, len(order)):
         spread(i)
-    side.append(side_swap(side_sum(*summed[1], *far)))
+    side = [side_swap(side_sum(*summed[chunk], *far[chunk])) for chunk in range(CHUNKS)]
     hit = place_of[:, None] == jnp.arange(devices * slots, dtype=jnp.int32)[None, :]
     looked = jnp.dot(
         hit.astype(bf16), returned.reshape(devices * slots, channels), preferred_element_type=f32

time: 150 us -> 149 us (level)
  blocking collectives: 11.9 us -> 0 us
  starting transfers between devices: 26.2 us -> 34.2 us
  local copies, waits for them, and re-layouts: 12.6 us -> 15.3 us
    all_to_all x1 -> x0, blocking collectives: 11.9 us -> none  [per_device(): wanted = lax.all_to_all(requests, axes, 0, 0, tiled=True)[:, :slots]]
    all_to_all x1 -> x2, starting transfers between devices: 3.44 us -> 12.2 us  [the longest x1 7.33 us: per_device(): wanted = lax.all_to_all(requests, axes, 0, 0, tiled=True)[:, :slots]]
    unnamed x47 -> x51, local copies, waits for them, and re-layouts: 6.78 us -> 8.81 us
  transfers between devices with their start and end apart: 32 -> 33, of which waited for: 15 -> 11; matrix products, arithmetic and copies ran while one was open for 6% -> 5% of each run, Pallas kernels for 36% -> 37%
where the time goes in v2:
time: 149 us
  Pallas kernels  56.9 us (38%)
  waiting for transfers between devices  37.6 us (25%)
  starting transfers between devices  34.2 us (23%)
  local copies, waits for them, and re-layouts  15.3 us (10%)
  other arithmetic  2.94 us (2%)
    ppermute x31, waiting for transfers between devices, swap(): lax.ppermute(v, 'member', [(i, i ^ 1 << bit) for i in range(members)])  37.6 us
    pallas_call x2, Pallas kernels, mlp_chunk(): pl.pallas_call(functools.partial(mlp_body, order=order, first=chunk * cou...  32.2 us
    ppermute x31, starting transfers between devices, swap(): lax.ppermute(v, 'member', [(i, i ^ 1 << bit) for i in range(members)])  22 us
    unnamed x51, local copies, waits for them, and re-layouts  8.81 us
    pallas_call x2, Pallas kernels, ple_chunk(): pl.pallas_call(functools.partial(ple_body, order=order), out_shape=jax.Sh...  7.96 us
    pallas_call x3, Pallas kernels, place(): pl.pallas_call(functools.partial(place_body, plan=plan, count=count, alia...  7.6 us
    all_to_all x1, starting transfers between devices, per_device(): wanted = lax.all_to_all(requests, axes, 0, 0, tiled=True)[:, :slots]  7.33 us
    pallas_call x2, Pallas kernels, side_sum(): pl.pallas_call(side_body, out_shape=(out, out), grid=(2,), in_specs=[bloc...  5.25 us
  transfers between devices with their start and end apart: 33, of which 11 were waited for; matrix products, arithmetic and copies ran while one was open for 5% of the time, Pallas kernels for 37%

profile of v2, /device:TPU:0, one launch (start us, length us, event | category | flops | bytes accessed | tf_op | source)
XLA Modules:
  0.0 148.7 jit_solution(12370213426656631945)
XLA Ops:
  2.5 7.3 %all-to-all-start = ((s32[32,1,128]{2,1,0:T(1,128)}), s32[32,1,128]{2,1,0:T(1,128)S(1)}, u32[]{:S(2)}, u32[]{:S(2)}) async-start(s32[32,1,128]{2,1,0:T(1,128)} %bitcast.12), calls=%async_computation | async-start | bytes 32768 | tf_op jit(solution)/shard_map/all_to_all | solution.py:392
  10.8 1.8 %collective-permute-start = (bf16[1,2,32,2048]{3,2,1,0:T(8,128)(2,1)S(1)}, bf16[1,2,32,2048]{3,2,1,0:T(8,128)(2,1)S(1)}, u32[]{:S(2)}, u32[]{:S(2)}) collective-permute-start(bf16[1,2,32,2048]{3,2,1,0:T(8,128)(2,1)S(1)} %maximum_bitcast_fusion), channel_id=1, source_target_pairs={{0,4},{1,5},{2,6},{3,7},{4,0},{5,1},{6,2},{7,3},{8,12},{9,13},{10,... | collective-permute-start | bytes 786440 | tf_op jit(solution)/shard_map/ppermute | solution.py:364
  13.4 16.2 %mlp.2 = (bf16[4,96,2048]{2,1,0:T(8,128)(2,1)S(1)}, bf16[4,96,2048]{2,1,0:T(8,128)(2,1)}) custom-call(s32[1]{0:T(128)} %bitcast.me, bf16[8,192,2048]{2,1,0:T(8,128)(2,1)} %bitcast.29, f32[1,2048]{1,0:T(1,128)S(1)} %slice_bitcast_fusion.gains, bf16[2048,1024]{1,0:T(8,128)(2,1)} %bitcast.36, bf16[2048,1024]{1,0:T(8,128)(2,1)} %bitcast.38, ...), custom_call_target="tpu_custom_call" | custom-call | flops 9663676416 | bytes 12582912 | tf_op jit(solution)/shard_map/mlp/pallas_call | solution.py:111
  30.8 4.9 %gather_fusion = bf16[512,256]{1,0:T(8,128)(2,1)} fusion(bf16[8192,256]{1,0:T(8,128)(2,1)} %param.15, s32[1024]{0:T(1024)S(1)} %pad_clamp_fusion), kind=kCustom, calls=%fused_computation | custom fusion | bytes 526336 | tf_op jit(solution)/shard_map/jit(_take)/gather | solution.py:396
  35.8 16.0 %mlp.3 = (bf16[4,96,2048]{2,1,0:T(8,128)(2,1)S(1)}, bf16[4,96,2048]{2,1,0:T(8,128)(2,1)}) custom-call(s32[1]{0:T(128)} %bitcast.me, bf16[8,192,2048]{2,1,0:T(8,128)(2,1)} %bitcast.30, f32[1,2048]{1,0:T(1,128)S(1)} %slice_bitcast_fusion.gains, bf16[2048,1024]{1,0:T(8,128)(2,1)} %bitcast.37, bf16[2048,1024]{1,0:T(8,128)(2,1)} %bitcast.39, ...), custom_call_target="tpu_custom_call" | custom-call | flops 9663676416 | bytes 12582912 | tf_op jit(solution)/shard_map/mlp/pallas_call | solution.py:111
  55.0 12.4 %collective-permute-done.6 = bf16[2,2,32,2048]{3,2,1,0:T(8,128)(2,1)S(1)} collective-permute-done((bf16[2,2,32,2048]{3,2,1,0:T(8,128)(2,1)S(1)}, bf16[2,2,32,2048]{3,2,1,0:T(8,128)(2,1)S(1)}, u32[]{:S(2)}, u32[]{:S(2)}) %collective-permute-start.6) | collective-permute-done | bytes 524320 | tf_op jit(solution)/shard_map/ppermute | solution.py:364
  67.5 4.9 %all-to-all-start.1 = ((bf16[32,16,256]{2,1,0:T(8,128)(2,1)}), bf16[32,16,256]{2,1,0:T(8,128)(2,1)}, u32[]{:S(2)}, u32[]{:S(2)}) async-start(bf16[32,16,256]{2,1,0:T(8,128)(2,1)} %bitcast.14), calls=%async_computation.1 | async-start | bytes 524288 | tf_op jit(solution)/shard_map/all_to_all | solution.py:397
  72.4 2.0 %far.3 = (bf16[96,1024]{1,0:T(8,128)(2,1)}, bf16[96,1024]{1,0:T(8,128)(2,1)}) custom-call(bf16[4,96,2048]{2,1,0:T(8,128)(2,1)} %copy-done.2, bf16[4,96,2048]{2,1,0:T(8,128)(2,1)} %collective-permute-done.14.recv.recv_x.recv_y), custom_call_target="tpu_custom_call" | custom-call | flops 196608 | bytes 1179648 | tf_op jit(solution)/shard_map/far/pallas_call | solution.py:220
  74.4 1.7 %collective-permute-start.15 = (bf16[96,1024]{1,0:T(8,128)(2,1)}, bf16[96,1024]{1,0:T(8,128)(2,1)S(1)}, u32[]{:S(2)}, u32[]{:S(2)}) collective-permute-start(bf16[96,1024]{1,0:T(8,128)(2,1)} %get-tuple-element.31), channel_id=1, source_target_pairs={{0,2},{1,3},{2,0},{3,1},{4,6},{5,7},{6,4},{7,5},{8,10},{9,11},{10,... | collective-permute-start | bytes 589832 | tf_op jit(solution)/shard_map/ppermute | solution.py:364
  78.7 1.9 %far.2 = (bf16[96,1024]{1,0:T(8,128)(2,1)}, bf16[96,1024]{1,0:T(8,128)(2,1)}) custom-call(bf16[4,96,2048]{2,1,0:T(8,128)(2,1)} %copy-done, bf16[4,96,2048]{2,1,0:T(8,128)(2,1)} %copy-done.8), custom_call_target="tpu_custom_call" | custom-call | flops 196608 | bytes 1179648 | tf_op jit(solution)/shard_map/far/pallas_call | solution.py:220
  81.5 1.6 %collective-permute-done.15.low = bf16[96,1024]{1,0:T(8,128)(2,1)S(1)} collective-permute-done((bf16[96,1024]{1,0:T(8,128)(2,1)}, bf16[96,1024]{1,0:T(8,128)(2,1)S(1)}, u32[]{:S(2)}, u32[]{:S(2)}) %collective-permute-start.15) | collective-permute-done | bytes 196640 | tf_op jit(solution)/shard_map/ppermute | solution.py:364
  83.1 1.5 %collective-permute-done.16.high = bf16[96,1024]{1,0:T(8,128)(2,1)} collective-permute-done((bf16[96,1024]{1,0:T(8,128)(2,1)}, bf16[96,1024]{1,0:T(8,128)(2,1)}, u32[]{:S(2)}, u32[]{:S(2)}) %collective-permute-start.16) | collective-permute-done | bytes 196640 | tf_op jit(solution)/shard_map/ppermute | solution.py:364
  84.7 2.6 %side.3 = (bf16[96,2048]{1,0:T(8,128)(2,1)}, bf16[96,2048]{1,0:T(8,128)(2,1)}) custom-call(bf16[4,96,2048]{2,1,0:T(8,128)(2,1)} %copy-done.2, bf16[4,96,2048]{2,1,0:T(8,128)(2,1)} %collective-permute-done.14.recv.recv_x.recv_y, bf16[4,96,2048]{2,1,0:T(8,128)(2,1)} %copy-done.2, bf16[4,96,2048]{2,1,0:T(8,128)(2,1)} %collective-permute-done.14.recv.recv_x.recv_y, ...), custom_call_target="tpu_custom_call" | custom-call | flops 589824 | bytes 2752512 | tf_op jit(solution)/shard_map/side/pallas_call | solution.py:256
  91.0 2.6 %side.2 = (bf16[96,2048]{1,0:T(8,128)(2,1)}, bf16[96,2048]{1,0:T(8,128)(2,1)}) custom-call(bf16[4,96,2048]{2,1,0:T(8,128)(2,1)} %copy-done, bf16[4,96,2048]{2,1,0:T(8,128)(2,1)} %copy-done.8, bf16[4,96,2048]{2,1,0:T(8,128)(2,1)} %copy-done, bf16[4,96,2048]{2,1,0:T(8,128)(2,1)} %copy-done.8, bf16[96,1024]{1,0:T(8,128)(2,1)} %copy-done.21, ...), custom_call_target="tpu_custom_call" | custom-call | flops 589824 | bytes 2752512 | tf_op jit(solution)/shard_map/side/pallas_call | solution.py:256
  96.6 2.9 %collective-permute-done.17.from_x = bf16[96,2048]{1,0:T(8,128)(2,1)S(1)} collective-permute-done((bf16[96,2048]{1,0:T(8,128)(2,1)}, bf16[96,2048]{1,0:T(8,128)(2,1)S(1)}, u32[]{:S(2)}, u32[]{:S(2)}) %collective-permute-start.17) | collective-permute-done | bytes 393248 | tf_op jit(solution)/shard_map/ppermute | solution.py:364
  101.4 4.2 %ple.3.refs_0_ = bf16[96,2048]{1,0:T(8,128)(2,1)S(1)} custom-call(s32[1]{0:T(128)} %bitcast.me, bf16[4,96,2048]{2,1,0:T(8,128)(2,1)S(1)} %copy-done.3, bf16[4,96,2048]{2,1,0:T(8,128)(2,1)} %collective-permute-done.14.recv.recv_x.recv_y, bf16[96,2048]{1,0:T(8,128)(2,1)S(1)} %copy-done.7, bf16[96,2048]{1,0:T(8,128)(2,1)} %collective-permute-done.18.from_y, ...), custom_call_target="tpu_custom_call" | custom-call | flops 201326592 | bytes 2097152 | tf_op jit(solution)/shard_map/ple/pallas_call | solution.py:180
  108.6 3.8 %ple.2.refs_4_ = bf16[96,2048]{1,0:T(8,128)(2,1)S(1)} custom-call(s32[1]{0:T(128)} %bitcast.me, bf16[4,96,2048]{2,1,0:T(8,128)(2,1)S(1)} %copy-done.1, bf16[4,96,2048]{2,1,0:T(8,128)(2,1)} %copy-done.8, bf16[96,2048]{1,0:T(8,128)(2,1)S(1)} %collective-permute-done.4.from_x, bf16[96,2048]{1,0:T(8,128)(2,1)} %collective-permute-done.5.from_y, ...), custom_call_target="tpu_custom_call" | custom-call | flops 201326592 | bytes 2097152 | tf_op jit(solution)/shard_map/ple/pallas_call | solution.py:180
  115.9 7.8 %collective-permute-done.10.refs_5_ = bf16[96,2048]{1,0:T(8,128)(2,1)S(1)} collective-permute-done((bf16[96,2048]{1,0:T(8,128)(2,1)S(1)}, bf16[96,2048]{1,0:T(8,128)(2,1)S(1)}, u32[]{:S(2)}, u32[]{:S(2)}) %collective-permute-start.10) | collective-permute-done | bytes 393248 | tf_op jit(solution)/shard_map/ppermute | solution.py:364
  125.1 4.7 %collective-permute-done.20.refs_0_ = bf16[96,1024]{1,0:T(8,128)(2,1)S(1)} collective-permute-done((bf16[96,1024]{1,0:T(8,128)(2,1)S(1)}, bf16[96,1024]{1,0:T(8,128)(2,1)S(1)}, u32[]{:S(2)}, u32[]{:S(2)}) %collective-permute-start.20) | collective-permute-done | bytes 196640 | tf_op jit(solution)/shard_map/ppermute | solution.py:364
  133.4 3.7 %collective-permute-done.9.refs_0_ = bf16[96,1024]{1,0:T(8,128)(2,1)} collective-permute-done((bf16[96,1024]{1,0:T(8,128)(2,1)S(1)}, bf16[96,1024]{1,0:T(8,128)(2,1)}, u32[]{:S(2)}, u32[]{:S(2)}) %collective-permute-start.9) | collective-permute-done | bytes 196640 | tf_op jit(solution)/shard_map/ppermute | solution.py:364
  137.2 2.1 %collective-permute-done.11.refs_1_ = bf16[96,1024]{1,0:T(8,128)(2,1)} collective-permute-done((bf16[96,1024]{1,0:T(8,128)(2,1)S(1)}, bf16[96,1024]{1,0:T(8,128)(2,1)}, u32[]{:S(2)}, u32[]{:S(2)}) %collective-permute-start.11) | collective-permute-done | bytes 196640 | tf_op jit(solution)/shard_map/ppermute | solution.py:364
  139.3 2.5 %place.3.refs_10_ = bf16[8,192,2048]{2,1,0:T(8,128)(2,1)} custom-call(s32[1]{0:T(128)} %bitcast.me, bf16[96,2048]{1,0:T(8,128)(2,1)} %copy-done.4, bf16[96,2048]{1,0:T(8,128)(2,1)} %copy-done.9, bf16[96,2048]{1,0:T(8,128)(2,1)} %copy-done.10, bf16[96,2048]{1,0:T(8,128)(2,1)} %copy-done.13, bf16[96,2048]{1,0:T(8,128)(2,1)} %copy-done.14, ...), custom_call_target="tpu_custom_call" | custom-call | tf_op jit(solution)/shard_map/place/pallas_call | solution.py:300
  143.4 3.1 %place.4.refs_4_ = bf16[8,192,2048]{2,1,0:T(8,128)(2,1)} custom-call(s32[1]{0:T(128)} %bitcast.me, bf16[96,1024]{1,0:T(8,128)(2,1)} %copy-done.19, bf16[96,1024]{1,0:T(8,128)(2,1)} %collective-permute-done.22.refs_1_, bf16[96,1024]{1,0:T(8,128)(2,1)} %copy-done.20, ...), custom_call_target="tpu_custom_call", output_to_operand_aliasing={{}: (11, {})} | custom-call | tf_op jit(solution)/shard_map/place/pallas_call | solution.py:300
  146.5 2.0 %place.5 = bf16[8,192,2048]{2,1,0:T(8,128)(2,1)} custom-call(s32[1]{0:T(128)} %bitcast.me, bf16[96,1024]{1,0:T(8,128)(2,1)} %collective-permute-done.9.refs_0_, bf16[96,1024]{1,0:T(8,128)(2,1)} %collective-permute-done.11.refs_1_, bf16[96,1024]{1,0:T(8,128)(2,1)} %collective-permute-done.12.refs_2_, ...), custom_call_target="tpu_custom_call", output_to_operand_aliasing={{}: (5, {})} | custom-call | tf_op jit(solution)/shard_map/place/pallas_call | solution.py:300
  (122 shorter events, 33.8 us)
Async XLA Ops:
  2.5 28.3 %all-to-all-start = ((s32[32,1,128]{2,1,0:T(1,128)}), s32[32,1,128]{2,1,0:T(1,128)S(1)}, u32[]{:S(2)}, u32[]{:S(2)}) async-start(s32[32,1,128]{2,1,0:T(1,128)} %bitcast.12), calls=%async_computation | async-start | bytes 32768 | tf_op jit(solution)/shard_map/all_to_all | solution.py:392
  10.8 24.9 %collective-permute-start = (bf16[1,2,32,2048]{3,2,1,0:T(8,128)(2,1)S(1)}, bf16[1,2,32,2048]{3,2,1,0:T(8,128)(2,1)S(1)}, u32[]{:S(2)}, u32[]{:S(2)}) collective-permute-start(bf16[1,2,32,2048]{3,2,1,0:T(8,128)(2,1)S(1)} %maximum_bitcast_fusion), channel_id=1, source_target_pairs={{0,4},{1,5},{2,6},{3,7},{4,0},{5,1},{6,2},{7,3},{8,12},{9,13},{10,... | collective-permute-start | bytes 786440 | tf_op jit(solution)/shard_map/ppermute | solution.py:364
  30.7 41.7 %collective-permute-start.14 = (bf16[4,96,2048]{2,1,0:T(8,128)(2,1)}, bf16[4,96,2048]{2,1,0:T(8,128)(2,1)}, u32[]{:S(2)}, u32[]{:S(2)}) collective-permute-start(bf16[4,96,2048]{2,1,0:T(8,128)(2,1)} %get-tuple-element.30), channel_id=1, source_target_pairs={{0,1},{1,0},{2,3},{3,2},{4,5},{5,4},{6,7},{7,6},{8,9},{9,8},{10,11... | collective-permute-start | bytes 4718600 | tf_op jit(solution)/shard_map/ppermute | solution.py:364
  53.0 24.5 %collective-permute-start.1 = (bf16[4,96,2048]{2,1,0:T(8,128)(2,1)}, bf16[4,96,2048]{2,1,0:T(8,128)(2,1)S(1)}, u32[]{:S(2)}, u32[]{:S(2)}) collective-permute-start(bf16[4,96,2048]{2,1,0:T(8,128)(2,1)} %get-tuple-element.25), channel_id=1, source_target_pairs={{0,1},{1,0},{2,3},{3,2},{4,5},{5,4},{6,7},{7,6},{8,9},{9,8},{10,11... | collective-permute-start | bytes 4718600 | tf_op jit(solution)/shard_map/ppermute | solution.py:364
  53.5 13.8 %collective-permute-start.6 = (bf16[2,2,32,2048]{3,2,1,0:T(8,128)(2,1)S(1)}, bf16[2,2,32,2048]{3,2,1,0:T(8,128)(2,1)S(1)}, u32[]{:S(2)}, u32[]{:S(2)}) collective-permute-start(bf16[2,2,32,2048]{3,2,1,0:T(8,128)(2,1)S(1)} %pad_maximum_fusion.1), channel_id=1, source_target_pairs={{0,2},{1,3},{2,0},{3,1},{4,6},{5,7},{6,4},{7,5},{8,10},{9,11},{10,... | collective-permute-start | bytes 1572872 | tf_op jit(solution)/shard_map/ppermute | solution.py:364
  67.5 29.2 %collective-permute-start.7 = (bf16[4,2,32,2048]{3,2,1,0:T(8,128)(2,1)S(1)}, bf16[4,2,32,2048]{3,2,1,0:T(8,128)(2,1)}, u32[]{:S(2)}, u32[]{:S(2)}) collective-permute-start(bf16[4,2,32,2048]{3,2,1,0:T(8,128)(2,1)S(1)} %pad_maximum_fusion.mine), channel_id=1, source_target_pairs={{0,1},{1,0},{2,3},{3,2},{4,5},{5,4},{6,7},{7,6},{8,9},{9,8},{10,11... | collective-permute-start | bytes 3145736 | tf_op jit(solution)/shard_map/ppermute | solution.py:364
  67.5 27.9 %all-to-all-start.1 = ((bf16[32,16,256]{2,1,0:T(8,128)(2,1)}), bf16[32,16,256]{2,1,0:T(8,128)(2,1)}, u32[]{:S(2)}, u32[]{:S(2)}) async-start(bf16[32,16,256]{2,1,0:T(8,128)(2,1)} %bitcast.14), calls=%async_computation.1 | async-start | bytes 524288 | tf_op jit(solution)/shard_map/all_to_all | solution.py:397
  74.4 8.7 %collective-permute-start.15 = (bf16[96,1024]{1,0:T(8,128)(2,1)}, bf16[96,1024]{1,0:T(8,128)(2,1)S(1)}, u32[]{:S(2)}, u32[]{:S(2)}) collective-permute-start(bf16[96,1024]{1,0:T(8,128)(2,1)} %get-tuple-element.31), channel_id=1, source_target_pairs={{0,2},{1,3},{2,0},{3,1},{4,6},{5,7},{6,4},{7,5},{8,10},{9,11},{10,... | collective-permute-start | bytes 589832 | tf_op jit(solution)/shard_map/ppermute | solution.py:364
  76.1 8.6 %collective-permute-start.16 = (bf16[96,1024]{1,0:T(8,128)(2,1)}, bf16[96,1024]{1,0:T(8,128)(2,1)}, u32[]{:S(2)}, u32[]{:S(2)}) collective-permute-start(bf16[96,1024]{1,0:T(8,128)(2,1)} %get-tuple-element.32), channel_id=1, source_target_pairs={{0,4},{1,5},{2,6},{3,7},{4,0},{5,1},{6,2},{7,3},{8,12},{9,13},{10,... | collective-permute-start | bytes 589832 | tf_op jit(solution)/shard_map/ppermute | solution.py:364
  80.6 9.0 %collective-permute-start.2 = (bf16[96,1024]{1,0:T(8,128)(2,1)}, bf16[96,1024]{1,0:T(8,128)(2,1)S(1)}, u32[]{:S(2)}, u32[]{:S(2)}) collective-permute-start(bf16[96,1024]{1,0:T(8,128)(2,1)} %get-tuple-element.26), channel_id=1, source_target_pairs={{0,2},{1,3},{2,0},{3,1},{4,6},{5,7},{6,4},{7,5},{8,10},{9,11},{10,... | collective-permute-start | bytes 589832 | tf_op jit(solution)/shard_map/ppermute | solution.py:364
  81.2 8.4 %collective-permute-start.3 = (bf16[96,1024]{1,0:T(8,128)(2,1)}, bf16[96,1024]{1,0:T(8,128)(2,1)S(1)}, u32[]{:S(2)}, u32[]{:S(2)}) collective-permute-start(bf16[96,1024]{1,0:T(8,128)(2,1)} %get-tuple-element.27), channel_id=1, source_target_pairs={{0,4},{1,5},{2,6},{3,7},{4,0},{5,1},{6,2},{7,3},{8,12},{9,13},{10,... | collective-permute-start | bytes 589832 | tf_op jit(solution)/shard_map/ppermute | solution.py:364
  87.3 12.3 %collective-permute-start.17 = (bf16[96,2048]{1,0:T(8,128)(2,1)}, bf16[96,2048]{1,0:T(8,128)(2,1)S(1)}, u32[]{:S(2)}, u32[]{:S(2)}) collective-permute-start(bf16[96,2048]{1,0:T(8,128)(2,1)} %get-tuple-element.33), channel_id=1, source_target_pairs={{0,2},{1,3},{2,0},{3,1},{4,6},{5,7},{6,4},{7,5},{8,10},{9,11},{10,... | collective-permute-start | bytes 1179656 | tf_op jit(solution)/shard_map/ppermute | solution.py:364
  88.1 12.3 %collective-permute-start.18 = (bf16[96,2048]{1,0:T(8,128)(2,1)}, bf16[96,2048]{1,0:T(8,128)(2,1)}, u32[]{:S(2)}, u32[]{:S(2)}) collective-permute-start(bf16[96,2048]{1,0:T(8,128)(2,1)} %get-tuple-element.34), channel_id=1, source_target_pairs={{0,4},{1,5},{2,6},{3,7},{4,0},{5,1},{6,2},{7,3},{8,12},{9,13},{10,... | collective-permute-start | bytes 1179656 | tf_op jit(solution)/shard_map/ppermute | solution.py:364
  93.6 14.8 %collective-permute-start.4 = (bf16[96,2048]{1,0:T(8,128)(2,1)}, bf16[96,2048]{1,0:T(8,128)(2,1)S(1)}, u32[]{:S(2)}, u32[]{:S(2)}) collective-permute-start(bf16[96,2048]{1,0:T(8,128)(2,1)} %get-tuple-element.28), channel_id=1, source_target_pairs={{0,2},{1,3},{2,0},{3,1},{4,6},{5,7},{6,4},{7,5},{8,10},{9,11},{10,... | collective-permute-start | bytes 1179656 | tf_op jit(solution)/shard_map/ppermute | solution.py:364
  94.9 13.7 %collective-permute-start.5 = (bf16[96,2048]{1,0:T(8,128)(2,1)}, bf16[96,2048]{1,0:T(8,128)(2,1)}, u32[]{:S(2)}, u32[]{:S(2)}) collective-permute-start(bf16[96,2048]{1,0:T(8,128)(2,1)} %get-tuple-element.29), channel_id=1, source_target_pairs={{0,4},{1,5},{2,6},{3,7},{4,0},{5,1},{6,2},{7,3},{8,12},{9,13},{10,... | collective-permute-start | bytes 1179656 | tf_op jit(solution)/shard_map/ppermute | solution.py:364
  105.6 9.6 %collective-permute-start.21 = (bf16[96,2048]{1,0:T(8,128)(2,1)S(1)}, bf16[96,2048]{1,0:T(8,128)(2,1)S(1)}, u32[]{:S(2)}, u32[]{:S(2)}) collective-permute-start(bf16[96,2048]{1,0:T(8,128)(2,1)S(1)} %ple.3.refs_0_), channel_id=1, source_target_pairs={{0,2},{1,3},{2,0},{3,1},{4,6},{5,7},{6,4},{7,5},{8,10},{9,11},{10,... | collective-permute-start | bytes 1179656 | tf_op jit(solution)/shard_map/ppermute | solution.py:364
  112.5 11.2 %collective-permute-start.10 = (bf16[96,2048]{1,0:T(8,128)(2,1)S(1)}, bf16[96,2048]{1,0:T(8,128)(2,1)S(1)}, u32[]{:S(2)}, u32[]{:S(2)}) collective-permute-start(bf16[96,2048]{1,0:T(8,128)(2,1)S(1)} %ple.2.refs_4_), channel_id=1, source_target_pairs={{0,2},{1,3},{2,0},{3,1},{4,6},{5,7},{6,4},{7,5},{8,10},{9,11},{10,... | collective-permute-start | bytes 1179656 | tf_op jit(solution)/shard_map/ppermute | solution.py:364
  113.7 10.7 %collective-permute-start.8 = (bf16[96,2048]{1,0:T(8,128)(2,1)S(1)}, bf16[96,2048]{1,0:T(8,128)(2,1)S(1)}, u32[]{:S(2)}, u32[]{:S(2)}) collective-permute-start(bf16[96,2048]{1,0:T(8,128)(2,1)S(1)} %ple.2.refs_4_), channel_id=1, source_target_pairs={{0,4},{1,5},{2,6},{3,7},{4,0},{5,1},{6,2},{7,3},{8,12},{9,13},{10,... | collective-permute-start | bytes 1179656 | tf_op jit(solution)/shard_map/ppermute | solution.py:364
  115.3 16.4 %collective-permute-start.25 = (bf16[96,2048]{1,0:T(8,128)(2,1)S(1)}, bf16[96,2048]{1,0:T(8,128)(2,1)S(1)}, u32[]{:S(2)}, u32[]{:S(2)}) collective-permute-start(bf16[96,2048]{1,0:T(8,128)(2,1)S(1)} %ple.2.refs_4_), channel_id=1, source_target_pairs={{0,1},{1,0},{2,3},{3,2},{4,5},{5,4},{6,7},{7,6},{8,9},{9,8},{10,11... | collective-permute-start | bytes 1179656 | tf_op jit(solution)/shard_map/ppermute | solution.py:364
  115.3 16.4 %collective-permute-start.29 = (bf16[96,2048]{1,0:T(8,128)(2,1)S(1)}, bf16[96,2048]{1,0:T(8,128)(2,1)S(1)}, u32[]{:S(2)}, u32[]{:S(2)}) collective-permute-start(bf16[96,2048]{1,0:T(8,128)(2,1)S(1)} %collective-permute-done.21.refs_1_), channel_id=1, source_target_pairs={{0,1},{1,0},{2,3},{3,2},{4,5},{5,4},{6,7},{7,6},{8,9},{9,8},{10,11... | collective-permute-start | bytes 1179656 | tf_op jit(solution)/shard_map/ppermute | solution.py:364
  115.8 16.5 %collective-permute-start.30 = (bf16[96,2048]{1,0:T(8,128)(2,1)S(1)}, bf16[96,2048]{1,0:T(8,128)(2,1)S(1)}, u32[]{:S(2)}, u32[]{:S(2)}) collective-permute-start(bf16[96,2048]{1,0:T(8,128)(2,1)S(1)} %collective-permute-done.19.refs_2_), channel_id=1, source_target_pairs={{0,1},{1,0},{2,3},{3,2},{4,5},{5,4},{6,7},{7,6},{8,9},{9,8},{10,11... | collective-permute-start | bytes 1179656 | tf_op jit(solution)/shard_map/ppermute | solution.py:364
  131.6 10.2 %collective-permute-start.26 = (bf16[96,2048]{1,0:T(8,128)(2,1)S(1)}, bf16[96,2048]{1,0:T(8,128)(2,1)S(1)}, u32[]{:S(2)}, u32[]{:S(2)}) collective-permute-start(bf16[96,2048]{1,0:T(8,128)(2,1)S(1)} %collective-permute-done.10.refs_5_), channel_id=1, source_target_pairs={{0,1},{1,0},{2,3},{3,2},{4,5},{5,4},{6,7},{7,6},{8,9},{9,8},{10,11... | collective-permute-start | bytes 1179656 | tf_op jit(solution)/shard_map/ppermute | solution.py:364
  131.7 10.1 %collective-permute-start.27 = (bf16[96,2048]{1,0:T(8,128)(2,1)S(1)}, bf16[96,2048]{1,0:T(8,128)(2,1)S(1)}, u32[]{:S(2)}, u32[]{:S(2)}) collective-permute-start(bf16[96,2048]{1,0:T(8,128)(2,1)S(1)} %collective-permute-done.8.refs_6_), channel_id=1, source_target_pairs={{0,1},{1,0},{2,3},{3,2},{4,5},{5,4},{6,7},{7,6},{8,9},{9,8},{10,11... | collective-permute-start | bytes 1179656 | tf_op jit(solution)/shard_map/ppermute | solution.py:364
  137.2 9.3 %collective-permute-start.12 = (bf16[96,1024]{1,0:T(8,128)(2,1)}, bf16[96,1024]{1,0:T(8,128)(2,1)}, u32[]{:S(2)}, u32[]{:S(2)}) collective-permute-start(bf16[96,1024]{1,0:T(8,128)(2,1)} %collective-permute-done.9.refs_0_), channel_id=1, source_target_pairs={{0,1},{1,0},{2,3},{3,2},{4,5},{5,4},{6,7},{7,6},{8,9},{9,8},{10,11... | collective-permute-start | bytes 589832 | tf_op jit(solution)/shard_map/ppermute | solution.py:364
  (34 other events, 259.8 us)

commit v3 on v2

--- a/solution.py
+++ b/solution.py
@@ -60,11 +60,8 @@
 
     for i in range(members):
         fetch(i).start()
-    for j in range(tiles):
-        for copy in weights(j):
-            copy.start()
-    for j in range(out_tiles):
-        down(j).start()
+    for copy in weights(0):
+        copy.start()
     for i in range(members):
         fetch(i).wait()
         rows[i] = norm_rows(rows[i].astype(jnp.float32), gains[...]).astype(jnp.bfloat16)
@@ -73,6 +70,12 @@
     for j in range(tiles):
         for copy in weights(j):
             copy.wait()
+        if j == 0:
+            for later in range(1, tiles):
+                for copy in weights(later):
+                    copy.start()
+            for later in range(out_tiles):
+                down(later).start()
         for part in range(parts):
             x = rows[part * per : (part + 1) * per].reshape(size, rows.shape[2])
             gate = jnp.dot(x, gate_w[j], preferred_element_type=jnp.float32)

time: 149 us -> 147 us (0.987)
  Pallas kernels: 56.9 us -> 54.8 us
    pallas_call x2, Pallas kernels: 32.2 us -> 30.1 us  [mlp_chunk(): pl.pallas_call(functools.partial(mlp_body, order=order, first=chunk * cou...]
  transfers between devices with their start and end apart: 33 -> 33, of which waited for: 11 -> 11; matrix products, arithmetic and copies ran while one was open for 5% -> 6% of each run, Pallas kernels for 37% -> 36%
where the time goes in v3:
time: 147 us
  Pallas kernels  54.8 us (37%)
  waiting for transfers between devices  37.6 us (26%)
  starting transfers between devices  34.2 us (23%)
  local copies, waits for them, and re-layouts  15.3 us (10%)
  other arithmetic  2.94 us (2%)
    ppermute x31, waiting for transfers between devices, swap(): lax.ppermute(v, 'member', [(i, i ^ 1 << bit) for i in range(members)])  37.6 us
    pallas_call x2, Pallas kernels, mlp_chunk(): pl.pallas_call(functools.partial(mlp_body, order=order, first=chunk * cou...  30.1 us
    ppermute x31, starting transfers between devices, swap(): lax.ppermute(v, 'member', [(i, i ^ 1 << bit) for i in range(members)])  22 us
    unnamed x51, local copies, waits for them, and re-layouts  8.81 us
    pallas_call x2, Pallas kernels, ple_chunk(): pl.pallas_call(functools.partial(ple_body, order=order), out_shape=jax.Sh...  7.96 us
    pallas_call x3, Pallas kernels, place(): pl.pallas_call(functools.partial(place_body, plan=plan, count=count, alia...  7.6 us
    all_to_all x1, starting transfers between devices, per_device(): wanted = lax.all_to_all(requests, axes, 0, 0, tiled=True)[:, :slots]  7.33 us
    pallas_call x2, Pallas kernels, side_sum(): pl.pallas_call(side_body, out_shape=(out, out), grid=(2,), in_specs=[bloc...  5.25 us
  transfers between devices with their start and end apart: 33, of which 11 were waited for; matrix products, arithmetic and copies ran while one was open for 6% of the time, Pallas kernels for 36%

profile of v3, /device:TPU:0, one launch (start us, length us, event | category | flops | bytes accessed | tf_op | source)
XLA Modules:
  0.0 146.6 jit_solution(6175968201245426777)
XLA Ops:
  2.5 7.3 %all-to-all-start = ((s32[32,1,128]{2,1,0:T(1,128)}), s32[32,1,128]{2,1,0:T(1,128)S(1)}, u32[]{:S(2)}, u32[]{:S(2)}) async-start(s32[32,1,128]{2,1,0:T(1,128)} %bitcast.12), calls=%async_computation | async-start | bytes 32768 | tf_op jit(solution)/shard_map/all_to_all | solution.py:395
  10.8 1.8 %collective-permute-start = (bf16[1,2,32,2048]{3,2,1,0:T(8,128)(2,1)S(1)}, bf16[1,2,32,2048]{3,2,1,0:T(8,128)(2,1)S(1)}, u32[]{:S(2)}, u32[]{:S(2)}) collective-permute-start(bf16[1,2,32,2048]{3,2,1,0:T(8,128)(2,1)S(1)} %maximum_bitcast_fusion), channel_id=1, source_target_pairs={{0,4},{1,5},{2,6},{3,7},{4,0},{5,1},{6,2},{7,3},{8,12},{9,13},{10,... | collective-permute-start | bytes 786440 | tf_op jit(solution)/shard_map/ppermute | solution.py:367
  13.4 15.1 %mlp.2 = (bf16[4,96,2048]{2,1,0:T(8,128)(2,1)S(1)}, bf16[4,96,2048]{2,1,0:T(8,128)(2,1)}) custom-call(s32[1]{0:T(128)} %bitcast.me, bf16[8,192,2048]{2,1,0:T(8,128)(2,1)} %bitcast.29, f32[1,2048]{1,0:T(1,128)S(1)} %slice_bitcast_fusion.gains, bf16[2048,1024]{1,0:T(8,128)(2,1)} %bitcast.36, bf16[2048,1024]{1,0:T(8,128)(2,1)} %bitcast.38, ...), custom_call_target="tpu_custom_call" | custom-call | flops 9663676416 | bytes 12582912 | tf_op jit(solution)/shard_map/mlp/pallas_call | solution.py:114
  29.7 4.9 %gather_fusion = bf16[512,256]{1,0:T(8,128)(2,1)} fusion(bf16[8192,256]{1,0:T(8,128)(2,1)} %param.15, s32[1024]{0:T(1024)S(1)} %pad_clamp_fusion), kind=kCustom, calls=%fused_computation | custom fusion | bytes 526336 | tf_op jit(solution)/shard_map/jit(_take)/gather | solution.py:399
  34.7 15.0 %mlp.3 = (bf16[4,96,2048]{2,1,0:T(8,128)(2,1)S(1)}, bf16[4,96,2048]{2,1,0:T(8,128)(2,1)}) custom-call(s32[1]{0:T(128)} %bitcast.me, bf16[8,192,2048]{2,1,0:T(8,128)(2,1)} %bitcast.30, f32[1,2048]{1,0:T(1,128)S(1)} %slice_bitcast_fusion.gains, bf16[2048,1024]{1,0:T(8,128)(2,1)} %bitcast.37, bf16[2048,1024]{1,0:T(8,128)(2,1)} %bitcast.39, ...), custom_call_target="tpu_custom_call" | custom-call | flops 9663676416 | bytes 12582912 | tf_op jit(solution)/shard_map/mlp/pallas_call | solution.py:114
  52.9 12.4 %collective-permute-done.6 = bf16[2,2,32,2048]{3,2,1,0:T(8,128)(2,1)S(1)} collective-permute-done((bf16[2,2,32,2048]{3,2,1,0:T(8,128)(2,1)S(1)}, bf16[2,2,32,2048]{3,2,1,0:T(8,128)(2,1)S(1)}, u32[]{:S(2)}, u32[]{:S(2)}) %collective-permute-start.6) | collective-permute-done | bytes 524320 | tf_op jit(solution)/shard_map/ppermute | solution.py:367
  65.4 4.9 %all-to-all-start.1 = ((bf16[32,16,256]{2,1,0:T(8,128)(2,1)}), bf16[32,16,256]{2,1,0:T(8,128)(2,1)}, u32[]{:S(2)}, u32[]{:S(2)}) async-start(bf16[32,16,256]{2,1,0:T(8,128)(2,1)} %bitcast.14), calls=%async_computation.1 | async-start | bytes 524288 | tf_op jit(solution)/shard_map/all_to_all | solution.py:400
  70.3 2.0 %far.3 = (bf16[96,1024]{1,0:T(8,128)(2,1)}, bf16[96,1024]{1,0:T(8,128)(2,1)}) custom-call(bf16[4,96,2048]{2,1,0:T(8,128)(2,1)} %copy-done.2, bf16[4,96,2048]{2,1,0:T(8,128)(2,1)} %collective-permute-done.14.recv.recv_x.recv_y), custom_call_target="tpu_custom_call" | custom-call | flops 196608 | bytes 1179648 | tf_op jit(solution)/shard_map/far/pallas_call | solution.py:223
  72.3 1.7 %collective-permute-start.15 = (bf16[96,1024]{1,0:T(8,128)(2,1)}, bf16[96,1024]{1,0:T(8,128)(2,1)S(1)}, u32[]{:S(2)}, u32[]{:S(2)}) collective-permute-start(bf16[96,1024]{1,0:T(8,128)(2,1)} %get-tuple-element.31), channel_id=1, source_target_pairs={{0,2},{1,3},{2,0},{3,1},{4,6},{5,7},{6,4},{7,5},{8,10},{9,11},{10,... | collective-permute-start | bytes 589832 | tf_op jit(solution)/shard_map/ppermute | solution.py:367
  76.6 1.9 %far.2 = (bf16[96,1024]{1,0:T(8,128)(2,1)}, bf16[96,1024]{1,0:T(8,128)(2,1)}) custom-call(bf16[4,96,2048]{2,1,0:T(8,128)(2,1)} %copy-done, bf16[4,96,2048]{2,1,0:T(8,128)(2,1)} %copy-done.8), custom_call_target="tpu_custom_call" | custom-call | flops 196608 | bytes 1179648 | tf_op jit(solution)/shard_map/far/pallas_call | solution.py:223
  79.4 1.6 %collective-permute-done.15.low = bf16[96,1024]{1,0:T(8,128)(2,1)S(1)} collective-permute-done((bf16[96,1024]{1,0:T(8,128)(2,1)}, bf16[96,1024]{1,0:T(8,128)(2,1)S(1)}, u32[]{:S(2)}, u32[]{:S(2)}) %collective-permute-start.15) | collective-permute-done | bytes 196640 | tf_op jit(solution)/shard_map/ppermute | solution.py:367
  81.0 1.5 %collective-permute-done.16.high = bf16[96,1024]{1,0:T(8,128)(2,1)} collective-permute-done((bf16[96,1024]{1,0:T(8,128)(2,1)}, bf16[96,1024]{1,0:T(8,128)(2,1)}, u32[]{:S(2)}, u32[]{:S(2)}) %collective-permute-start.16) | collective-permute-done | bytes 196640 | tf_op jit(solution)/shard_map/ppermute | solution.py:367
  82.5 2.6 %side.3 = (bf16[96,2048]{1,0:T(8,128)(2,1)}, bf16[96,2048]{1,0:T(8,128)(2,1)}) custom-call(bf16[4,96,2048]{2,1,0:T(8,128)(2,1)} %copy-done.2, bf16[4,96,2048]{2,1,0:T(8,128)(2,1)} %collective-permute-done.14.recv.recv_x.recv_y, bf16[4,96,2048]{2,1,0:T(8,128)(2,1)} %copy-done.2, bf16[4,96,2048]{2,1,0:T(8,128)(2,1)} %collective-permute-done.14.recv.recv_x.recv_y, ...), custom_call_target="tpu_custom_call" | custom-call | flops 589824 | bytes 2752512 | tf_op jit(solution)/shard_map/side/pallas_call | solution.py:259
  88.9 2.6 %side.2 = (bf16[96,2048]{1,0:T(8,128)(2,1)}, bf16[96,2048]{1,0:T(8,128)(2,1)}) custom-call(bf16[4,96,2048]{2,1,0:T(8,128)(2,1)} %copy-done, bf16[4,96,2048]{2,1,0:T(8,128)(2,1)} %copy-done.8, bf16[4,96,2048]{2,1,0:T(8,128)(2,1)} %copy-done, bf16[4,96,2048]{2,1,0:T(8,128)(2,1)} %copy-done.8, bf16[96,1024]{1,0:T(8,128)(2,1)} %copy-done.21, ...), custom_call_target="tpu_custom_call" | custom-call | flops 589824 | bytes 2752512 | tf_op jit(solution)/shard_map/side/pallas_call | solution.py:259
  94.5 2.9 %collective-permute-done.17.from_x = bf16[96,2048]{1,0:T(8,128)(2,1)S(1)} collective-permute-done((bf16[96,2048]{1,0:T(8,128)(2,1)}, bf16[96,2048]{1,0:T(8,128)(2,1)S(1)}, u32[]{:S(2)}, u32[]{:S(2)}) %collective-permute-start.17) | collective-permute-done | bytes 393248 | tf_op jit(solution)/shard_map/ppermute | solution.py:367
  99.3 4.2 %ple.3.refs_0_ = bf16[96,2048]{1,0:T(8,128)(2,1)S(1)} custom-call(s32[1]{0:T(128)} %bitcast.me, bf16[4,96,2048]{2,1,0:T(8,128)(2,1)S(1)} %copy-done.3, bf16[4,96,2048]{2,1,0:T(8,128)(2,1)} %collective-permute-done.14.recv.recv_x.recv_y, bf16[96,2048]{1,0:T(8,128)(2,1)S(1)} %copy-done.7, bf16[96,2048]{1,0:T(8,128)(2,1)} %collective-permute-done.18.from_y, ...), custom_call_target="tpu_custom_call" | custom-call | flops 201326592 | bytes 2097152 | tf_op jit(solution)/shard_map/ple/pallas_call | solution.py:183
  106.5 3.8 %ple.2.refs_4_ = bf16[96,2048]{1,0:T(8,128)(2,1)S(1)} custom-call(s32[1]{0:T(128)} %bitcast.me, bf16[4,96,2048]{2,1,0:T(8,128)(2,1)S(1)} %copy-done.1, bf16[4,96,2048]{2,1,0:T(8,128)(2,1)} %copy-done.8, bf16[96,2048]{1,0:T(8,128)(2,1)S(1)} %collective-permute-done.4.from_x, bf16[96,2048]{1,0:T(8,128)(2,1)} %collective-permute-done.5.from_y, ...), custom_call_target="tpu_custom_call" | custom-call | flops 201326592 | bytes 2097152 | tf_op jit(solution)/shard_map/ple/pallas_call | solution.py:183
  113.8 7.8 %collective-permute-done.10.refs_5_ = bf16[96,2048]{1,0:T(8,128)(2,1)S(1)} collective-permute-done((bf16[96,2048]{1,0:T(8,128)(2,1)S(1)}, bf16[96,2048]{1,0:T(8,128)(2,1)S(1)}, u32[]{:S(2)}, u32[]{:S(2)}) %collective-permute-start.10) | collective-permute-done | bytes 393248 | tf_op jit(solution)/shard_map/ppermute | solution.py:367
  122.9 4.7 %collective-permute-done.20.refs_0_ = bf16[96,1024]{1,0:T(8,128)(2,1)S(1)} collective-permute-done((bf16[96,1024]{1,0:T(8,128)(2,1)S(1)}, bf16[96,1024]{1,0:T(8,128)(2,1)S(1)}, u32[]{:S(2)}, u32[]{:S(2)}) %collective-permute-start.20) | collective-permute-done | bytes 196640 | tf_op jit(solution)/shard_map/ppermute | solution.py:367
  131.3 3.8 %collective-permute-done.9.refs_0_ = bf16[96,1024]{1,0:T(8,128)(2,1)} collective-permute-done((bf16[96,1024]{1,0:T(8,128)(2,1)S(1)}, bf16[96,1024]{1,0:T(8,128)(2,1)}, u32[]{:S(2)}, u32[]{:S(2)}) %collective-permute-start.9) | collective-permute-done | bytes 196640 | tf_op jit(solution)/shard_map/ppermute | solution.py:367
  135.1 2.1 %collective-permute-done.11.refs_1_ = bf16[96,1024]{1,0:T(8,128)(2,1)} collective-permute-done((bf16[96,1024]{1,0:T(8,128)(2,1)S(1)}, bf16[96,1024]{1,0:T(8,128)(2,1)}, u32[]{:S(2)}, u32[]{:S(2)}) %collective-permute-start.11) | collective-permute-done | bytes 196640 | tf_op jit(solution)/shard_map/ppermute | solution.py:367
  137.2 2.5 %place.3.refs_10_ = bf16[8,192,2048]{2,1,0:T(8,128)(2,1)} custom-call(s32[1]{0:T(128)} %bitcast.me, bf16[96,2048]{1,0:T(8,128)(2,1)} %copy-done.4, bf16[96,2048]{1,0:T(8,128)(2,1)} %copy-done.9, bf16[96,2048]{1,0:T(8,128)(2,1)} %copy-done.10, bf16[96,2048]{1,0:T(8,128)(2,1)} %copy-done.13, bf16[96,2048]{1,0:T(8,128)(2,1)} %copy-done.14, ...), custom_call_target="tpu_custom_call" | custom-call | tf_op jit(solution)/shard_map/place/pallas_call | solution.py:303
  141.3 3.1 %place.4.refs_4_ = bf16[8,192,2048]{2,1,0:T(8,128)(2,1)} custom-call(s32[1]{0:T(128)} %bitcast.me, bf16[96,1024]{1,0:T(8,128)(2,1)} %copy-done.19, bf16[96,1024]{1,0:T(8,128)(2,1)} %collective-permute-done.22.refs_1_, bf16[96,1024]{1,0:T(8,128)(2,1)} %copy-done.20, ...), custom_call_target="tpu_custom_call", output_to_operand_aliasing={{}: (11, {})} | custom-call | tf_op jit(solution)/shard_map/place/pallas_call | solution.py:303
  144.4 2.0 %place.5 = bf16[8,192,2048]{2,1,0:T(8,128)(2,1)} custom-call(s32[1]{0:T(128)} %bitcast.me, bf16[96,1024]{1,0:T(8,128)(2,1)} %collective-permute-done.9.refs_0_, bf16[96,1024]{1,0:T(8,128)(2,1)} %collective-permute-done.11.refs_1_, bf16[96,1024]{1,0:T(8,128)(2,1)} %collective-permute-done.12.refs_2_, ...), custom_call_target="tpu_custom_call", output_to_operand_aliasing={{}: (5, {})} | custom-call | tf_op jit(solution)/shard_map/place/pallas_call | solution.py:303
  (122 shorter events, 33.8 us)
Async XLA Ops:
  2.5 27.1 %all-to-all-start = ((s32[32,1,128]{2,1,0:T(1,128)}), s32[32,1,128]{2,1,0:T(1,128)S(1)}, u32[]{:S(2)}, u32[]{:S(2)}) async-start(s32[32,1,128]{2,1,0:T(1,128)} %bitcast.12), calls=%async_computation | async-start | bytes 32768 | tf_op jit(solution)/shard_map/all_to_all | solution.py:395
  10.8 23.8 %collective-permute-start = (bf16[1,2,32,2048]{3,2,1,0:T(8,128)(2,1)S(1)}, bf16[1,2,32,2048]{3,2,1,0:T(8,128)(2,1)S(1)}, u32[]{:S(2)}, u32[]{:S(2)}) collective-permute-start(bf16[1,2,32,2048]{3,2,1,0:T(8,128)(2,1)S(1)} %maximum_bitcast_fusion), channel_id=1, source_target_pairs={{0,4},{1,5},{2,6},{3,7},{4,0},{5,1},{6,2},{7,3},{8,12},{9,13},{10,... | collective-permute-start | bytes 786440 | tf_op jit(solution)/shard_map/ppermute | solution.py:367
  29.6 40.7 %collective-permute-start.14 = (bf16[4,96,2048]{2,1,0:T(8,128)(2,1)}, bf16[4,96,2048]{2,1,0:T(8,128)(2,1)}, u32[]{:S(2)}, u32[]{:S(2)}) collective-permute-start(bf16[4,96,2048]{2,1,0:T(8,128)(2,1)} %get-tuple-element.30), channel_id=1, source_target_pairs={{0,1},{1,0},{2,3},{3,2},{4,5},{5,4},{6,7},{7,6},{8,9},{9,8},{10,11... | collective-permute-start | bytes 4718600 | tf_op jit(solution)/shard_map/ppermute | solution.py:367
  50.9 24.5 %collective-permute-start.1 = (bf16[4,96,2048]{2,1,0:T(8,128)(2,1)}, bf16[4,96,2048]{2,1,0:T(8,128)(2,1)S(1)}, u32[]{:S(2)}, u32[]{:S(2)}) collective-permute-start(bf16[4,96,2048]{2,1,0:T(8,128)(2,1)} %get-tuple-element.25), channel_id=1, source_target_pairs={{0,1},{1,0},{2,3},{3,2},{4,5},{5,4},{6,7},{7,6},{8,9},{9,8},{10,11... | collective-permute-start | bytes 4718600 | tf_op jit(solution)/shard_map/ppermute | solution.py:367
  51.4 13.8 %collective-permute-start.6 = (bf16[2,2,32,2048]{3,2,1,0:T(8,128)(2,1)S(1)}, bf16[2,2,32,2048]{3,2,1,0:T(8,128)(2,1)S(1)}, u32[]{:S(2)}, u32[]{:S(2)}) collective-permute-start(bf16[2,2,32,2048]{3,2,1,0:T(8,128)(2,1)S(1)} %pad_maximum_fusion.1), channel_id=1, source_target_pairs={{0,2},{1,3},{2,0},{3,1},{4,6},{5,7},{6,4},{7,5},{8,10},{9,11},{10,... | collective-permute-start | bytes 1572872 | tf_op jit(solution)/shard_map/ppermute | solution.py:367
  65.4 29.2 %collective-permute-start.7 = (bf16[4,2,32,2048]{3,2,1,0:T(8,128)(2,1)S(1)}, bf16[4,2,32,2048]{3,2,1,0:T(8,128)(2,1)}, u32[]{:S(2)}, u32[]{:S(2)}) collective-permute-start(bf16[4,2,32,2048]{3,2,1,0:T(8,128)(2,1)S(1)} %pad_maximum_fusion.mine), channel_id=1, source_target_pairs={{0,1},{1,0},{2,3},{3,2},{4,5},{5,4},{6,7},{7,6},{8,9},{9,8},{10,11... | collective-permute-start | bytes 3145736 | tf_op jit(solution)/shard_map/ppermute | solution.py:367
  65.4 27.9 %all-to-all-start.1 = ((bf16[32,16,256]{2,1,0:T(8,128)(2,1)}), bf16[32,16,256]{2,1,0:T(8,128)(2,1)}, u32[]{:S(2)}, u32[]{:S(2)}) async-start(bf16[32,16,256]{2,1,0:T(8,128)(2,1)} %bitcast.14), calls=%async_computation.1 | async-start | bytes 524288 | tf_op jit(solution)/shard_map/all_to_all | solution.py:400
  72.3 8.7 %collective-permute-start.15 = (bf16[96,1024]{1,0:T(8,128)(2,1)}, bf16[96,1024]{1,0:T(8,128)(2,1)S(1)}, u32[]{:S(2)}, u32[]{:S(2)}) collective-permute-start(bf16[96,1024]{1,0:T(8,128)(2,1)} %get-tuple-element.31), channel_id=1, source_target_pairs={{0,2},{1,3},{2,0},{3,1},{4,6},{5,7},{6,4},{7,5},{8,10},{9,11},{10,... | collective-permute-start | bytes 589832 | tf_op jit(solution)/shard_map/ppermute | solution.py:367
  74.0 8.6 %collective-permute-start.16 = (bf16[96,1024]{1,0:T(8,128)(2,1)}, bf16[96,1024]{1,0:T(8,128)(2,1)}, u32[]{:S(2)}, u32[]{:S(2)}) collective-permute-start(bf16[96,1024]{1,0:T(8,128)(2,1)} %get-tuple-element.32), channel_id=1, source_target_pairs={{0,4},{1,5},{2,6},{3,7},{4,0},{5,1},{6,2},{7,3},{8,12},{9,13},{10,... | collective-permute-start | bytes 589832 | tf_op jit(solution)/shard_map/ppermute | solution.py:367
  78.5 9.0 %collective-permute-start.2 = (bf16[96,1024]{1,0:T(8,128)(2,1)}, bf16[96,1024]{1,0:T(8,128)(2,1)S(1)}, u32[]{:S(2)}, u32[]{:S(2)}) collective-permute-start(bf16[96,1024]{1,0:T(8,128)(2,1)} %get-tuple-element.26), channel_id=1, source_target_pairs={{0,2},{1,3},{2,0},{3,1},{4,6},{5,7},{6,4},{7,5},{8,10},{9,11},{10,... | collective-permute-start | bytes 589832 | tf_op jit(solution)/shard_map/ppermute | solution.py:367
  79.1 8.4 %collective-permute-start.3 = (bf16[96,1024]{1,0:T(8,128)(2,1)}, bf16[96,1024]{1,0:T(8,128)(2,1)S(1)}, u32[]{:S(2)}, u32[]{:S(2)}) collective-permute-start(bf16[96,1024]{1,0:T(8,128)(2,1)} %get-tuple-element.27), channel_id=1, source_target_pairs={{0,4},{1,5},{2,6},{3,7},{4,0},{5,1},{6,2},{7,3},{8,12},{9,13},{10,... | collective-permute-start | bytes 589832 | tf_op jit(solution)/shard_map/ppermute | solution.py:367
  85.2 12.3 %collective-permute-start.17 = (bf16[96,2048]{1,0:T(8,128)(2,1)}, bf16[96,2048]{1,0:T(8,128)(2,1)S(1)}, u32[]{:S(2)}, u32[]{:S(2)}) collective-permute-start(bf16[96,2048]{1,0:T(8,128)(2,1)} %get-tuple-element.33), channel_id=1, source_target_pairs={{0,2},{1,3},{2,0},{3,1},{4,6},{5,7},{6,4},{7,5},{8,10},{9,11},{10,... | collective-permute-start | bytes 1179656 | tf_op jit(solution)/shard_map/ppermute | solution.py:367
  86.0 12.3 %collective-permute-start.18 = (bf16[96,2048]{1,0:T(8,128)(2,1)}, bf16[96,2048]{1,0:T(8,128)(2,1)}, u32[]{:S(2)}, u32[]{:S(2)}) collective-permute-start(bf16[96,2048]{1,0:T(8,128)(2,1)} %get-tuple-element.34), channel_id=1, source_target_pairs={{0,4},{1,5},{2,6},{3,7},{4,0},{5,1},{6,2},{7,3},{8,12},{9,13},{10,... | collective-permute-start | bytes 1179656 | tf_op jit(solution)/shard_map/ppermute | solution.py:367
  91.5 14.8 %collective-permute-start.4 = (bf16[96,2048]{1,0:T(8,128)(2,1)}, bf16[96,2048]{1,0:T(8,128)(2,1)S(1)}, u32[]{:S(2)}, u32[]{:S(2)}) collective-permute-start(bf16[96,2048]{1,0:T(8,128)(2,1)} %get-tuple-element.28), channel_id=1, source_target_pairs={{0,2},{1,3},{2,0},{3,1},{4,6},{5,7},{6,4},{7,5},{8,10},{9,11},{10,... | collective-permute-start | bytes 1179656 | tf_op jit(solution)/shard_map/ppermute | solution.py:367
  92.8 13.7 %collective-permute-start.5 = (bf16[96,2048]{1,0:T(8,128)(2,1)}, bf16[96,2048]{1,0:T(8,128)(2,1)}, u32[]{:S(2)}, u32[]{:S(2)}) collective-permute-start(bf16[96,2048]{1,0:T(8,128)(2,1)} %get-tuple-element.29), channel_id=1, source_target_pairs={{0,4},{1,5},{2,6},{3,7},{4,0},{5,1},{6,2},{7,3},{8,12},{9,13},{10,... | collective-permute-start | bytes 1179656 | tf_op jit(solution)/shard_map/ppermute | solution.py:367
  103.5 9.6 %collective-permute-start.21 = (bf16[96,2048]{1,0:T(8,128)(2,1)S(1)}, bf16[96,2048]{1,0:T(8,128)(2,1)S(1)}, u32[]{:S(2)}, u32[]{:S(2)}) collective-permute-start(bf16[96,2048]{1,0:T(8,128)(2,1)S(1)} %ple.3.refs_0_), channel_id=1, source_target_pairs={{0,2},{1,3},{2,0},{3,1},{4,6},{5,7},{6,4},{7,5},{8,10},{9,11},{10,... | collective-permute-start | bytes 1179656 | tf_op jit(solution)/shard_map/ppermute | solution.py:367
  110.3 11.2 %collective-permute-start.10 = (bf16[96,2048]{1,0:T(8,128)(2,1)S(1)}, bf16[96,2048]{1,0:T(8,128)(2,1)S(1)}, u32[]{:S(2)}, u32[]{:S(2)}) collective-permute-start(bf16[96,2048]{1,0:T(8,128)(2,1)S(1)} %ple.2.refs_4_), channel_id=1, source_target_pairs={{0,2},{1,3},{2,0},{3,1},{4,6},{5,7},{6,4},{7,5},{8,10},{9,11},{10,... | collective-permute-start | bytes 1179656 | tf_op jit(solution)/shard_map/ppermute | solution.py:367
  111.6 10.7 %collective-permute-start.8 = (bf16[96,2048]{1,0:T(8,128)(2,1)S(1)}, bf16[96,2048]{1,0:T(8,128)(2,1)S(1)}, u32[]{:S(2)}, u32[]{:S(2)}) collective-permute-start(bf16[96,2048]{1,0:T(8,128)(2,1)S(1)} %ple.2.refs_4_), channel_id=1, source_target_pairs={{0,4},{1,5},{2,6},{3,7},{4,0},{5,1},{6,2},{7,3},{8,12},{9,13},{10,... | collective-permute-start | bytes 1179656 | tf_op jit(solution)/shard_map/ppermute | solution.py:367
  113.1 16.4 %collective-permute-start.25 = (bf16[96,2048]{1,0:T(8,128)(2,1)S(1)}, bf16[96,2048]{1,0:T(8,128)(2,1)S(1)}, u32[]{:S(2)}, u32[]{:S(2)}) collective-permute-start(bf16[96,2048]{1,0:T(8,128)(2,1)S(1)} %ple.2.refs_4_), channel_id=1, source_target_pairs={{0,1},{1,0},{2,3},{3,2},{4,5},{5,4},{6,7},{7,6},{8,9},{9,8},{10,11... | collective-permute-start | bytes 1179656 | tf_op jit(solution)/shard_map/ppermute | solution.py:367
  113.2 16.4 %collective-permute-start.29 = (bf16[96,2048]{1,0:T(8,128)(2,1)S(1)}, bf16[96,2048]{1,0:T(8,128)(2,1)S(1)}, u32[]{:S(2)}, u32[]{:S(2)}) collective-permute-start(bf16[96,2048]{1,0:T(8,128)(2,1)S(1)} %collective-permute-done.21.refs_1_), channel_id=1, source_target_pairs={{0,1},{1,0},{2,3},{3,2},{4,5},{5,4},{6,7},{7,6},{8,9},{9,8},{10,11... | collective-permute-start | bytes 1179656 | tf_op jit(solution)/shard_map/ppermute | solution.py:367
  113.7 16.5 %collective-permute-start.30 = (bf16[96,2048]{1,0:T(8,128)(2,1)S(1)}, bf16[96,2048]{1,0:T(8,128)(2,1)S(1)}, u32[]{:S(2)}, u32[]{:S(2)}) collective-permute-start(bf16[96,2048]{1,0:T(8,128)(2,1)S(1)} %collective-permute-done.19.refs_2_), channel_id=1, source_target_pairs={{0,1},{1,0},{2,3},{3,2},{4,5},{5,4},{6,7},{7,6},{8,9},{9,8},{10,11... | collective-permute-start | bytes 1179656 | tf_op jit(solution)/shard_map/ppermute | solution.py:367
  129.5 10.2 %collective-permute-start.26 = (bf16[96,2048]{1,0:T(8,128)(2,1)S(1)}, bf16[96,2048]{1,0:T(8,128)(2,1)S(1)}, u32[]{:S(2)}, u32[]{:S(2)}) collective-permute-start(bf16[96,2048]{1,0:T(8,128)(2,1)S(1)} %collective-permute-done.10.refs_5_), channel_id=1, source_target_pairs={{0,1},{1,0},{2,3},{3,2},{4,5},{5,4},{6,7},{7,6},{8,9},{9,8},{10,11... | collective-permute-start | bytes 1179656 | tf_op jit(solution)/shard_map/ppermute | solution.py:367
  129.6 10.1 %collective-permute-start.27 = (bf16[96,2048]{1,0:T(8,128)(2,1)S(1)}, bf16[96,2048]{1,0:T(8,128)(2,1)S(1)}, u32[]{:S(2)}, u32[]{:S(2)}) collective-permute-start(bf16[96,2048]{1,0:T(8,128)(2,1)S(1)} %collective-permute-done.8.refs_6_), channel_id=1, source_target_pairs={{0,1},{1,0},{2,3},{3,2},{4,5},{5,4},{6,7},{7,6},{8,9},{9,8},{10,11... | collective-permute-start | bytes 1179656 | tf_op jit(solution)/shard_map/ppermute | solution.py:367
  135.1 9.3 %collective-permute-start.12 = (bf16[96,1024]{1,0:T(8,128)(2,1)}, bf16[96,1024]{1,0:T(8,128)(2,1)}, u32[]{:S(2)}, u32[]{:S(2)}) collective-permute-start(bf16[96,1024]{1,0:T(8,128)(2,1)} %collective-permute-done.9.refs_0_), channel_id=1, source_target_pairs={{0,1},{1,0},{2,3},{3,2},{4,5},{5,4},{6,7},{7,6},{8,9},{9,8},{10,11... | collective-permute-start | bytes 589832 | tf_op jit(solution)/shard_map/ppermute | solution.py:367
  (34 other events, 259.8 us)
